TPU v7x, 32 devices: a whole 2x2x4 slice. The times are simulated.
32 devices in a mesh: w: 4 (over z), h: 8 (over y, x, core).
Axes of the slice: x: 2, y: 2, z: 4, core: 2. Of those that a mesh axis runs over, the one named last changes fastest.
Arguments:
- x: bfloat16 [1, 256, 1024, 128], P(None, 'h', 'w')
- w1: bfloat16 [3, 3, 128, 128], replicated
- gamma: float32 [128], replicated
- beta: float32 [128], replicated
- w2: bfloat16 [3, 3, 128, 128], replicated
- g: bfloat16 [1, 256, 1024, 128], P(None, 'h', 'w')
Outputs:
- output 1: bfloat16 [1, 256, 1024, 128], P(None, 'h', 'w')
- output 2: bfloat16 [1, 256, 1024, 128], P(None, 'h', 'w')
- output 3: float32 [3, 3, 128, 128], replicated
- output 4: float32 [3, 3, 128, 128], replicated
- output 5: float32 [128], replicated
- output 6: float32 [128], replicated
All inputs are finite; a program needn't handle non-finite values.
Results may differ from a plain program's by a relative error of at most 0.00104032.
Values are sent between devices in bfloat16 or wider.
A program may use at most 1 GiB of HBM per device.

v0:
```python
import jax
import jax.numpy as jnp
from jax import lax
from jax.sharding import PartitionSpec as P

GROUPS = 32
EPS = 1e-5
DN = ('NHWC', 'HWIO', 'NHWC')


def _conv(up, w):
    return lax.conv_general_dilated(up, w, (1, 1), 'VALID', dimension_numbers=DN, preferred_element_type=jnp.float32)


def _flip_t(w):
    return jnp.flip(w, (0, 1)).transpose(0, 1, 3, 2)


def _wgrad(up, v):
    th, tw = v.shape[1], v.shape[2]
    return jnp.stack([jnp.stack([jnp.einsum('bhwc,bhwo->co', up[:, a:a + th, b:b + tw], v, preferred_element_type=jnp.float32) for b in range(3)]) for a in range(3)])


def _edge(u, axis, name, n):
    lo = lax.slice_in_dim(u, 0, 1, axis=axis)
    hi = lax.slice_in_dim(u, u.shape[axis] - 1, u.shape[axis], axis=axis)
    if n == 1:
        prev = jnp.zeros_like(lo)
        nxt = jnp.zeros_like(lo)
    else:
        prev = lax.ppermute(hi, name, [(i, i + 1) for i in range(n - 1)])
        nxt = lax.ppermute(lo, name, [(i + 1, i) for i in range(n - 1)])
    return jnp.concatenate([prev, u, nxt], axis=axis)


def solution(mesh):
    nh, nw = mesh.shape['h'], mesh.shape['w']
    tile = P(None, 'h', 'w', None)

    def halo(u):
        return _edge(_edge(u, 1, 'h', nh), 2, 'w', nw)

    def body(x, w1, gamma, beta, w2, g):
        nb, th, tw, c = x.shape
        cg = c // GROUPS
        cnt = th * nh * tw * nw * cg
        xp = halo(x)
        a = _conv(xp, w1).astype(jnp.bfloat16).astype(jnp.float32)
        s = jnp.stack([a.sum((1, 2)), (a * a).sum((1, 2))])
        s = lax.psum(s.reshape(2, nb, GROUPS, cg).sum(-1), ('h', 'w')) / cnt
        rstd_g = lax.rsqrt(s[1] - s[0] * s[0] + EPS)
        mean = jnp.repeat(s[0], cg, axis=-1)[:, None, None, :]
        rstd = jnp.repeat(rstd_g, cg, axis=-1)[:, None, None, :]
        xhatv = (a - mean) * rstd
        zf, gelu_vjp = jax.vjp(lambda n: jax.nn.gelu(n, approximate=True), xhatv * gamma + beta)
        z = zf.astype(jnp.bfloat16)
        zp = halo(z)
        y = (_conv(zp, w2) + x.astype(jnp.float32)).astype(jnp.bfloat16)
        gp = halo(g)
        dz = _conv(gp, _flip_t(w2))
        dw2 = lax.psum(_wgrad(zp, g), ('h', 'w'))
        (dn,) = gelu_vjp(dz)
        t = lax.psum(jnp.stack([(dn * xhatv).sum((1, 2)), dn.sum((1, 2))]), ('h', 'w'))
        dgamma = t[0].sum(0)
        dbeta = t[1].sum(0)
        u = jnp.repeat((t * gamma).reshape(2, nb, GROUPS, cg).sum(-1) / cnt, cg, axis=-1)[:, :, None, None, :]
        da = (rstd * (dn * gamma - u[1] - xhatv * u[0])).astype(jnp.bfloat16)
        dap = halo(da)
        dx = (_conv(dap, _flip_t(w1)) + g.astype(jnp.float32)).astype(jnp.bfloat16)
        dw1 = lax.psum(_wgrad(xp, da), ('h', 'w'))
        return y, dx, dw1, dw2, dgamma, dbeta

    return jax.shard_map(body, mesh=mesh, in_specs=(tile, P(), P(), P(), P(), tile), out_specs=(tile, tile, P(), P(), P(), P()), check_vma=False)
```

profile of v0, /device:TPU:0, one launch (start us, length us, event | category | flops | bytes accessed | tf_op | source)
XLA Modules:
  0.0 460.9 jit_solution(6163050622079183932)
XLA Ops:
  7.2 3.3 copy.52
  10.6 2.4 collective-permute-start
  14.3 1.5 fusion.220
  15.8 5.7 %collective-permute-start.8 = (bf16[1,1,256,128]{3,2,1,0:T(8,128)(2,1)}, bf16[1,1,256,128]{3,2,1,0:T(8,128)(2,1)}, u32[]{:S(2)}, u32[]{:S(2)}) collective-permute-start(bf16[1,1,256,128]{3,2,1,0:T(8,128)(2,1)} %get-tuple-element.43), channel_id=1, source_target_pairs={{0,1},{1,2},{2,3},{3,4},{4,5},{5,6},{6,7},{8,9},{9,10},{10,11},{11... | collective-permute-start | bytes 196616 | tf_op jit(solution)/shard_map/ppermute | solution.py:31
  23.2 1.6 fusion.217
  24.8 1.7 copy.55
  26.5 3.5 collective-permute-start.2
  33.2 1.9 constant_dynamic-update-slice_fusion.1
  36.7 4.5 collective-permute-start.10
  43.2 2.1 copy.58
  45.4 5.3 %maximum_bitcast_fusion = bf16[34,1,258,128]{2,3,0,1:T(8,128)(2,1)} fusion(bf16[1,34,1,128]{2,3,1,0:T(8,128)(2,1)} %copy.58, bf16[1,1,256,128]{2,3,1,0:T(8,128)(2,1)} %copy-done.18, bf16[1,32,256,128]{2,3,1,0:T(8,128)(2,1)S(1)} %copy.52, bf16[1,1,256,128]{2,3,1,0:T(8,128)(2,1)} %copy-done.15, bf16[1,34,1,128]{2,3,1,0:T(8,128)(2,1)S(1)} %copy.57), kind=kLoop, calls=%fused_computation.42 | loop fusion | flops 11228160 | bytes 4491264 | tf_op jit(solution)/shard_map/concatenate | solution.py:33
  50.6 4.6 copy.106
  55.2 3.3 pad.clone
  58.5 4.6 %reshape.184 = bf16[34,1,8,33,128]{4,3,2,0,1:T(8,128)(2,1)} reshape(bf16[34,1,264,128]{3,2,0,1:T(8,128)(2,1)} %pad.clone) | data formatting | bytes 4595712 | tf_op jit(solution)/shard_map/conv_general_dilated | solution.py:12
  63.2 2.1 copy.61
  65.3 6.7 %fusion.10 = (f32[128]{0:T(128)S(1)}, f32[128]{0:T(128)S(1)}, bf16[32,8,33,128]{3,1,2,0:T(8,128)(2,1)}) fusion(pred[8,33]{0,1:T(8,128)(4,1)S(1)} %copy-done.44, bf16[3,3,128,128]{3,2,1,0:T(8,128)(2,1)S(1)} %copy-done, bf16[34,1,7,2,128]{4,2,3,0,1:T(8,128)(2,1)S(1)} %slice.200, bf16[34,1,8,33,128]{4,2,3,0,1:T(8,128)(2,1)S(1)} %copy.61), kind=kOutput, calls=%fused_computation.16 | convolution fusion | flops 2507378688 | bytes 4878600 | tf_op jit(solution)/shard_map/conv_general_dilated | solution.py:12
  72.4 44.6 %psum.28 = f32[2,1,32]{2,0,1:T(2,128)S(1)} all-reduce(f32[2,1,32]{2,0,1:T(2,128)S(1)} %bitcast.337), channel_id=1, replica_groups=mesh['w'=4,'h'=8] {'h','w'}, use_global_device_ids=true, to_apply=%region_3.0 | all-reduce | flops 64 | bytes 512 | tf_op jit(solution)/shard_map/psum | solution.py:50
  117.5 3.0 maximum_bitcast_fusion.2
  120.4 1.5 pad.4
  122.0 4.7 %reshape.202 = bf16[34,1,8,33,128]{4,3,2,0,1:T(8,128)(2,1)} reshape(bf16[34,1,264,128]{3,2,0,1:T(8,128)(2,1)} %pad.4) | data formatting | bytes 4595712 | tf_op jit(solution)/shard_map/conv_general_dilated | solution.py:12
  126.6 2.2 copy.80
  129.1 10.4 %fusion.27 = (f32[128]{0:T(128)S(1)}, f32[128]{0:T(128)S(1)}, f32[32,8,33,128]{3,1,2,0:T(8,128)}) fusion(bf16[32,8,33,128]{3,1,2,0:T(8,128)(2,1)S(1)} %copy-done.14, f32[128]{0:T(128)S(1)} %broadcast_in_dim.26, f32[128]{0:T(128)S(1)} %broadcast_in_dim.24, pred[8,33]{0,1:T(8,128)(4,1)S(1)} %copy-done.45, f32[128]{0:T(128)S(1)} %copy-done.41, ...), kind=kOutput, calls=%fused_computation.33 | convolution fusion | flops 2531168256 | bytes 9206024 | tf_op jit(solution)/shard_map/conv_general_dilated | solution.py:12
  139.5 41.9 %psum.29 = f32[2,1,128]{2,1,0:T(1,128)S(1)} all-reduce(f32[2,1,128]{2,1,0:T(1,128)S(1)} %pad_maximum_fusion.13), channel_id=1, replica_groups=mesh['w'=4,'h'=8] {'h','w'}, use_global_device_ids=true, to_apply=%region_6.7 | all-reduce | flops 256 | bytes 2048 | tf_op jit(solution)/shard_map/psum | solution.py:63
  182.0 5.0 %fusion.25 = (bf16[32,8,33,128]{3,1,2,0:T(8,128)(2,1)S(1)}, bf16[32,8,33,128]{3,1,2,0:T(8,128)(2,1)S(1)}) fusion(bf16[32,8,33,128]{3,1,2,0:T(8,128)(2,1)} %get-tuple-element.50, f32[32,8,33,128]{3,1,2,0:T(8,128)} %get-tuple-element.51, f32[128]{0:T(128)S(1)} %broadcast_in_dim.28, f32[128]{0:T(128)S(1)} %broadcast_in_dim.30, f32[128]{0:T(128)S(1)} %copy-done.39, ...), kind=kLoop, calls=%fused_computation.31 | loop fusion | flops 21626880 | bytes 10816512 | tf_op jit(solution)/shard_map/convert_element_type | solution.py:67
  189.7 3.3 maximum_maximum_fusion
  195.7 1.8 fusion.140
  197.5 1.8 fusion.146
  202.1 1.8 fusion.157
  203.9 2.1 copy.147
  206.5 1.7 slice.203
  208.2 3.0 copy.103
  211.4 1.6 collective-permute-start.4
  214.7 2.9 fusion.127
  218.3 6.2 %collective-permute-start.12 = (bf16[1,1,256,128]{3,2,1,0:T(8,128)(2,1)}, bf16[1,1,256,128]{3,2,1,0:T(8,128)(2,1)}, u32[]{:S(2)}, u32[]{:S(2)}) collective-permute-start(bf16[1,1,256,128]{3,2,1,0:T(8,128)(2,1)} %slice.214), channel_id=1, source_target_pairs={{0,1},{1,2},{2,3},{3,4},{4,5},{5,6},{6,7},{8,9},{9,10},{10,11},{11... | collective-permute-start | bytes 196616 | tf_op jit(solution)/shard_map/ppermute | solution.py:31
  225.1 1.5 collective-permute-start.13
  226.7 3.5 fusion.152
  233.4 1.6 fusion.216
  235.0 2.3 copy.70
  237.3 2.4 collective-permute-start.6
  243.6 4.5 collective-permute-start.14
  249.6 3.0 fusion.163
  255.4 2.1 copy.73
  257.5 4.0 maximum_maximum_fusion.1
  264.1 1.5 fusion.168
  265.6 1.5 fusion.174
  268.5 1.5 fusion.185
  270.1 2.8 maximum_bitcast_fusion.3
  272.9 1.6 pad.6
  274.5 4.8 %reshape.215 = bf16[34,1,8,33,128]{4,3,2,0,1:T(8,128)(2,1)} reshape(bf16[34,1,264,128]{3,2,0,1:T(8,128)(2,1)} %pad.6) | data formatting | bytes 4595712 | tf_op jit(solution)/shard_map/conv_general_dilated | solution.py:12
  279.3 2.1 copy.86
  281.5 5.2 %broadcast_select_fusion = f32[32,8,33,128]{3,1,2,0:T(8,128)S(1)} fusion(pred[8,33]{0,1:T(8,128)(4,1)S(1)} %copy-done.46, bf16[3,3,128,128]{3,2,1,0:T(8,128)(2,1)S(1)} %copy-done, bf16[34,1,7,2,128]{4,2,3,0,1:T(8,128)(2,1)S(1)} %slice.218, bf16[34,1,8,33,128]{4,2,3,0,1:T(8,128)(2,1)S(1)} %copy.86), kind=kOutput, calls=%fused_computation.76 | convolution fusion | flops 2499809280 | bytes 7040264 | tf_op jit(solution)/shard_map/conv_general_dilated | solution.py:12
  286.7 2.8 copy.87
  289.6 4.2 maximum_bitcast_fusion.1
  293.8 4.2 copy.107
  298.0 1.5 pad.2.clone
  299.6 3.5 reshape.197
  304.1 7.1 %broadcast_select_fusion.1 = f32[32,8,33,128]{3,1,2,0:T(8,128)} fusion(pred[8,33]{0,1:T(8,128)(4,1)S(1)} %copy-done.46, bf16[3,3,128,128]{3,2,1,0:T(8,128)(2,1)S(1)} %copy-done.43, bf16[34,1,7,2,128]{4,2,3,0,1:T(8,128)(2,1)S(1)} %slice.208, bf16[34,1,8,33,128]{4,2,3,0,1:T(8,128)(2,1)S(1)} %copy.76), kind=kOutput, calls=%fused_computation.77 | convolution fusion | flops 2499809280 | bytes 7040264 | tf_op jit(solution)/shard_map/conv_general_dilated | solution.py:12
  313.0 3.6 fusion.29
  316.6 2.1 copy.98
  318.7 3.2 copy.77
  323.3 2.1 copy.97
  325.5 124.3 %all-reduce.3.cloned.1.call-done = (f32[3,3,128,128]{3,2,1,0:T(8,128)}, f32[3,3,128,128]{3,2,1,0:T(8,128)}) async-done(((f32[3,3,128,128]{3,2,1,0:T(8,128)}, f32[3,3,128,128]{3,2,1,0:T(8,128)}), (f32[3,3,128,128]{3,2,1,0:T(8,128)}, f32[3,3,128,128]{3,2,1,0:T(8,128)})) %all-reduce.3.cloned.1.call-update) | async-done | bytes 1179664 | tf_op jit(solution)/shard_map/psum | solution.py:70
  449.8 1.9 copy.152
  451.7 1.9 copy.153
  (193 shorter events, 42.3 us)
Async XLA Ops:
  7.2 58.1 %copy-start = (bf16[3,3,128,128]{3,2,1,0:T(8,128)(2,1)S(1)}, bf16[3,3,128,128]{3,2,1,0:T(8,128)(2,1)}, u32[]{:S(2)}) copy-start(bf16[3,3,128,128]{3,2,1,0:T(8,128)(2,1)} %param.7) | copy-start | bytes 884740
  7.2 442.6 %all-reduce.3.cloned.1.call-start = ((), (), s32[]{:S(2)}) async-start(), calls=%async_computation | async-start | bytes 2359296 | tf_op jit(solution)/shard_map/psum | solution.py:70
  10.5 178.3 %copy-start.1 = (bf16[1,32,256,128]{2,3,1,0:T(8,128)(2,1)}, bf16[1,32,256,128]{2,3,1,0:T(8,128)(2,1)S(1)}, u32[]{:S(2)}) copy-start(bf16[1,32,256,128]{2,3,1,0:T(8,128)(2,1)S(1)} %copy.52) | copy-start | bytes 6291460
  10.6 12.3 %collective-permute-start = (bf16[1,1,256,128]{2,3,1,0:T(8,128)(2,1)S(1)}, bf16[1,1,256,128]{2,3,1,0:T(8,128)(2,1)S(1)}, u32[]{:S(2)}, u32[]{:S(2)}) collective-permute-start(bf16[1,1,256,128]{2,3,1,0:T(8,128)(2,1)S(1)} %get-tuple-element.44), channel_id=1, source_target_pairs={{0,1},{1,2},{2,3},{3,4},{4,5},{5,6},{6,7},{8,9},{9,10},{10,11},{11... | collective-permute-start | bytes 196616 | tf_op jit(solution)/shard_map/ppermute | solution.py:31
  13.0 9.9 %collective-permute-start.1 = (bf16[1,1,256,128]{2,3,1,0:T(8,128)(2,1)S(1)}, bf16[1,1,256,128]{2,3,1,0:T(8,128)(2,1)S(1)}, u32[]{:S(2)}, u32[]{:S(2)}) collective-permute-start(bf16[1,1,256,128]{2,3,1,0:T(8,128)(2,1)S(1)} %get-tuple-element.45), channel_id=1, source_target_pairs={{1,0},{2,1},{3,2},{4,3},{5,4},{6,5},{7,6},{9,8},{10,9},{11,10},{12... | collective-permute-start | bytes 196616 | tf_op jit(solution)/shard_map/ppermute | solution.py:32
  15.8 16.5 %collective-permute-start.8 = (bf16[1,1,256,128]{3,2,1,0:T(8,128)(2,1)}, bf16[1,1,256,128]{3,2,1,0:T(8,128)(2,1)}, u32[]{:S(2)}, u32[]{:S(2)}) collective-permute-start(bf16[1,1,256,128]{3,2,1,0:T(8,128)(2,1)} %get-tuple-element.43), channel_id=1, source_target_pairs={{0,1},{1,2},{2,3},{3,4},{4,5},{5,6},{6,7},{8,9},{9,10},{10,11},{11... | collective-permute-start | bytes 196616 | tf_op jit(solution)/shard_map/ppermute | solution.py:31
  21.6 13.6 %collective-permute-start.9 = (bf16[1,1,256,128]{3,2,1,0:T(8,128)(2,1)}, bf16[1,1,256,128]{3,2,1,0:T(8,128)(2,1)}, u32[]{:S(2)}, u32[]{:S(2)}) collective-permute-start(bf16[1,1,256,128]{3,2,1,0:T(8,128)(2,1)} %get-tuple-element.42), channel_id=1, source_target_pairs={{1,0},{2,1},{3,2},{4,3},{5,4},{6,5},{7,6},{9,8},{10,9},{11,10},{12... | collective-permute-start | bytes 196616 | tf_op jit(solution)/shard_map/ppermute | solution.py:32
  22.9 1.9 copy-start.15
  22.9 1.9 copy-start.18
  26.5 16.1 %collective-permute-start.2 = (bf16[1,34,1,128]{3,1,2,0:T(8,128)(2,1)S(1)}, bf16[1,34,1,128]{3,1,2,0:T(8,128)(2,1)S(1)}, u32[]{:S(2)}, u32[]{:S(2)}) collective-permute-start(bf16[1,34,1,128]{3,1,2,0:T(8,128)(2,1)S(1)} %copy.55), channel_id=1, source_target_pairs={{0,8},{8,16},{16,24},{1,9},{9,17},{17,25},{2,10},{10,18},{18,26},{... | collective-permute-start | bytes 26120 | tf_op jit(solution)/shard_map/ppermute | solution.py:31
  31.0 12.2 %collective-permute-start.3 = (bf16[1,34,1,128]{3,1,2,0:T(8,128)(2,1)}, bf16[1,34,1,128]{3,1,2,0:T(8,128)(2,1)}, u32[]{:S(2)}, u32[]{:S(2)}) collective-permute-start(bf16[1,34,1,128]{3,1,2,0:T(8,128)(2,1)} %copy.56), channel_id=1, source_target_pairs={{8,0},{16,8},{24,16},{9,1},{17,9},{25,17},{10,2},{18,10},{26,18},{... | collective-permute-start | bytes 26120 | tf_op jit(solution)/shard_map/ppermute | solution.py:32
  36.0 6.6 %copy-start.13 = (bf16[1,34,256,128]{3,2,1,0:T(8,128)(2,1)}, bf16[1,34,256,128]{3,2,1,0:T(8,128)(2,1)S(1)}, u32[]{:S(2)}) copy-start(bf16[1,34,256,128]{3,2,1,0:T(8,128)(2,1)S(1)} %constant_dynamic-update-slice_fusion) | copy-start | bytes 6684676
  36.7 80.7 %collective-permute-start.10 = (bf16[1,34,1,128]{3,2,1,0:T(2,128)(2,1)}, bf16[1,34,1,128]{3,2,1,0:T(2,128)(2,1)S(1)}, u32[]{:S(2)}, u32[]{:S(2)}) collective-permute-start(bf16[1,34,1,128]{3,2,1,0:T(2,128)(2,1)} %get-tuple-element.30), channel_id=1, source_target_pairs={{0,8},{8,16},{16,24},{1,9},{9,17},{17,25},{2,10},{10,18},{18,26},{... | collective-permute-start | bytes 26120 | tf_op jit(solution)/shard_map/ppermute | solution.py:31
  41.3 76.2 %collective-permute-start.11 = (bf16[1,34,1,128]{3,2,1,0:T(2,128)(2,1)}, bf16[1,34,1,128]{3,2,1,0:T(2,128)(2,1)}, u32[]{:S(2)}, u32[]{:S(2)}) collective-permute-start(bf16[1,34,1,128]{3,2,1,0:T(2,128)(2,1)} %get-tuple-element.31), channel_id=1, source_target_pairs={{8,0},{16,8},{24,16},{9,1},{17,9},{25,17},{10,2},{18,10},{26,18},{... | collective-permute-start | bytes 26120 | tf_op jit(solution)/shard_map/ppermute | solution.py:32
  63.2 2.2 copy-start.44
  117.4 11.5 %copy-start.40 = (f32[128]{0:T(128)}, f32[128]{0:T(128)S(1)}, u32[]{:S(2)}) copy-start(f32[128]{0:T(128)S(1)} %broadcast_in_dim.26) | copy-start | bytes 1540
  126.6 2.4 copy-start.14
  126.6 2.4 copy-start.39
  126.6 2.4 copy-start.41
  126.6 2.5 copy-start.42
  126.6 2.5 copy-start.45
  188.5 1.3 copy-start.7
  188.5 1.2 copy-start.16
  188.5 1.2 copy-start.19
  189.7 14.1 %copy-start.9 = (bf16[32,1,256,128]{3,0,2,1:T(8,128)(2,1)}, bf16[32,1,256,128]{3,0,2,1:T(8,128)(2,1)S(1)}, u32[]{:S(2)}) copy-start(bf16[32,1,256,128]{3,0,2,1:T(8,128)(2,1)S(1)} %slice.215) | copy-start | bytes 6291460
  197.5 1.8 copy-start.11
  208.2 3.0 copy-start.29
  208.2 4.9 %copy-start.28 = (bf16[1,8,33,128]{3,1,2,0:T(8,128)(2,1)S(1)}, bf16[1,8,33,128]{3,1,2,0:T(8,128)(2,1)}, u32[]{:S(2)}) copy-start(bf16[1,8,33,128]{3,1,2,0:T(8,128)(2,1)} %get-tuple-element.52) | copy-start | bytes 202756
  211.4 6.2 %copy-start.27 = (bf16[1,8,33,128]{3,1,2,0:T(8,128)(2,1)S(1)}, bf16[1,8,33,128]{3,1,2,0:T(8,128)(2,1)}, u32[]{:S(2)}) copy-start(bf16[1,8,33,128]{3,1,2,0:T(8,128)(2,1)} %get-tuple-element.38) | copy-start | bytes 202756
  211.4 21.1 %collective-permute-start.4 = (bf16[1,1,256,128]{2,3,1,0:T(8,128)(2,1)S(1)}, bf16[1,1,256,128]{2,3,1,0:T(8,128)(2,1)S(1)}, u32[]{:S(2)}, u32[]{:S(2)}) collective-permute-start(bf16[1,1,256,128]{2,3,1,0:T(8,128)(2,1)S(1)} %copy.102), channel_id=1, source_target_pairs={{0,1},{1,2},{2,3},{3,4},{4,5},{5,6},{6,7},{8,9},{9,10},{10,11},{11... | collective-permute-start | bytes 196616 | tf_op jit(solution)/shard_map/ppermute | solution.py:31
  213.1 11.3 %copy-start.26 = (bf16[1,8,33,128]{3,1,2,0:T(8,128)(2,1)S(1)}, bf16[1,8,33,128]{3,1,2,0:T(8,128)(2,1)}, u32[]{:S(2)}) copy-start(bf16[1,8,33,128]{3,1,2,0:T(8,128)(2,1)} %get-tuple-element.39) | copy-start | bytes 202756
  213.3 13.4 %copy-start.20 = (bf16[1,1,256,128]{2,3,1,0:T(8,128)(2,1)S(1)}, bf16[1,1,256,128]{2,3,1,0:T(8,128)(2,1)}, u32[]{:S(2)}) copy-start(bf16[1,1,256,128]{2,3,1,0:T(8,128)(2,1)} %copy-done.18) | copy-start | bytes 196612
  213.3 19.2 %collective-permute-start.5 = (bf16[1,1,256,128]{2,3,1,0:T(8,128)(2,1)S(1)}, bf16[1,1,256,128]{2,3,1,0:T(8,128)(2,1)S(1)}, u32[]{:S(2)}, u32[]{:S(2)}) collective-permute-start(bf16[1,1,256,128]{2,3,1,0:T(8,128)(2,1)S(1)} %copy.104), channel_id=1, source_target_pairs={{1,0},{2,1},{3,2},{4,3},{5,4},{6,5},{7,6},{9,8},{10,9},{11,10},{12... | collective-permute-start | bytes 196616 | tf_op jit(solution)/shard_map/ppermute | solution.py:32
  218.3 23.8 %collective-permute-start.12 = (bf16[1,1,256,128]{3,2,1,0:T(8,128)(2,1)}, bf16[1,1,256,128]{3,2,1,0:T(8,128)(2,1)}, u32[]{:S(2)}, u32[]{:S(2)}) collective-permute-start(bf16[1,1,256,128]{3,2,1,0:T(8,128)(2,1)} %slice.214), channel_id=1, source_target_pairs={{0,1},{1,2},{2,3},{3,4},{4,5},{5,6},{6,7},{8,9},{9,10},{10,11},{11... | collective-permute-start | bytes 196616 | tf_op jit(solution)/shard_map/ppermute | solution.py:31
  225.1 5.1 %copy-start.2 = (bf16[1,32,256,128]{2,3,1,0:T(8,128)(2,1)S(1)}, bf16[1,32,256,128]{2,3,1,0:T(8,128)(2,1)}, u32[]{:S(2)}) copy-start(bf16[1,32,256,128]{2,3,1,0:T(8,128)(2,1)} %copy-done.1) | copy-start | bytes 6291460
  225.1 5.1 %copy-start.10 = (bf16[32,1,256,128]{3,0,2,1:T(8,128)(2,1)S(1)}, bf16[32,1,256,128]{3,0,2,1:T(8,128)(2,1)}, u32[]{:S(2)}) copy-start(bf16[32,1,256,128]{3,0,2,1:T(8,128)(2,1)} %copy-done.9) | copy-start | bytes 6291460
  225.1 5.1 %copy-start.17 = (bf16[1,1,256,128]{2,3,1,0:T(8,128)(2,1)S(1)}, bf16[1,1,256,128]{2,3,1,0:T(8,128)(2,1)}, u32[]{:S(2)}) copy-start(bf16[1,1,256,128]{2,3,1,0:T(8,128)(2,1)} %copy-done.15) | copy-start | bytes 196612
  225.1 17.0 %collective-permute-start.13 = (bf16[1,1,256,128]{3,2,1,0:T(8,128)(2,1)}, bf16[1,1,256,128]{3,2,1,0:T(8,128)(2,1)}, u32[]{:S(2)}, u32[]{:S(2)}) collective-permute-start(bf16[1,1,256,128]{3,2,1,0:T(8,128)(2,1)} %slice.217), channel_id=1, source_target_pairs={{1,0},{2,1},{3,2},{4,3},{5,4},{6,5},{7,6},{9,8},{10,9},{11,10},{12... | collective-permute-start | bytes 196616 | tf_op jit(solution)/shard_map/ppermute | solution.py:32
  232.5 0.6 copy-start.21
  232.5 0.6 copy-start.23
  237.3 16.7 %collective-permute-start.6 = (bf16[1,34,1,128]{3,1,2,0:T(8,128)(2,1)}, bf16[1,34,1,128]{3,1,2,0:T(8,128)(2,1)}, u32[]{:S(2)}, u32[]{:S(2)}) collective-permute-start(bf16[1,34,1,128]{3,1,2,0:T(8,128)(2,1)} %copy.70), channel_id=1, source_target_pairs={{0,8},{8,16},{16,24},{1,9},{9,17},{17,25},{2,10},{10,18},{18,26},{... | collective-permute-start | bytes 26120 | tf_op jit(solution)/shard_map/ppermute | solution.py:31
  240.8 14.5 %collective-permute-start.7 = (bf16[1,34,1,128]{3,1,2,0:T(8,128)(2,1)}, bf16[1,34,1,128]{3,1,2,0:T(8,128)(2,1)}, u32[]{:S(2)}, u32[]{:S(2)}) collective-permute-start(bf16[1,34,1,128]{3,1,2,0:T(8,128)(2,1)} %copy.71), channel_id=1, source_target_pairs={{8,0},{16,8},{24,16},{9,1},{17,9},{25,17},{10,2},{18,10},{26,18},{... | collective-permute-start | bytes 26120 | tf_op jit(solution)/shard_map/ppermute | solution.py:32
  243.6 26.4 %collective-permute-start.14 = (bf16[1,34,1,128]{3,2,1,0:T(2,128)(2,1)}, bf16[1,34,1,128]{3,2,1,0:T(2,128)(2,1)S(1)}, u32[]{:S(2)}, u32[]{:S(2)}) collective-permute-start(bf16[1,34,1,128]{3,2,1,0:T(2,128)(2,1)} %get-tuple-element.28), channel_id=1, source_target_pairs={{0,8},{8,16},{16,24},{1,9},{9,17},{17,25},{2,10},{10,18},{18,26},{... | collective-permute-start | bytes 26120 | tf_op jit(solution)/shard_map/ppermute | solution.py:31
  248.2 4.5 copy-start.3
  248.2 4.5 copy-start.24
  248.2 21.8 %collective-permute-start.15 = (bf16[1,34,1,128]{3,2,1,0:T(2,128)(2,1)S(1)}, bf16[1,34,1,128]{3,2,1,0:T(2,128)(2,1)}, u32[]{:S(2)}, u32[]{:S(2)}) collective-permute-start(bf16[1,34,1,128]{3,2,1,0:T(2,128)(2,1)S(1)} %get-tuple-element.29), channel_id=1, source_target_pairs={{8,0},{16,8},{24,16},{9,1},{17,9},{25,17},{10,2},{18,10},{26,18},{... | collective-permute-start | bytes 26120 | tf_op jit(solution)/shard_map/ppermute | solution.py:32
  257.5 4.0 copy-start.4
  268.5 1.6 copy-start.6
  279.3 2.2 copy-start.46
  286.7 2.9 copy-start.8
  286.7 2.9 copy-start.22
  286.7 2.9 copy-start.25
  303.0 1.0 copy-start.43
  304.0 7.1 %copy-start.32 = (f32[1,128,128]{2,1,0:T(8,128)S(1)}, f32[1,128,128]{2,1,0:T(8,128)}, u32[]{:S(2)}) copy-start(f32[1,128,128]{2,1,0:T(8,128)} %fusion.163) | copy-start | bytes 196612
  304.0 7.1 %copy-start.37 = (f32[1,128,128]{2,1,0:T(8,128)S(1)}, f32[1,128,128]{2,1,0:T(8,128)}, u32[]{:S(2)}) copy-start(f32[1,128,128]{2,1,0:T(8,128)} %fusion.160) | copy-start | bytes 196612
  304.0 7.2 %copy-start.38 = (f32[1,128,128]{2,1,0:T(8,128)S(1)}, f32[1,128,128]{2,1,0:T(8,128)}, u32[]{:S(2)}) copy-start(f32[1,128,128]{2,1,0:T(8,128)} %fusion.168) | copy-start | bytes 196612
  304.0 7.2 %copy-start.30 = (f32[1,128,128]{2,1,0:T(8,128)S(1)}, f32[1,128,128]{2,1,0:T(8,128)}, u32[]{:S(2)}) copy-start(f32[1,128,128]{2,1,0:T(8,128)} %fusion.127) | copy-start | bytes 196612
  304.0 7.2 %copy-start.33 = (f32[1,128,128]{2,1,0:T(8,128)S(1)}, f32[1,128,128]{2,1,0:T(8,128)}, u32[]{:S(2)}) copy-start(f32[1,128,128]{2,1,0:T(8,128)} %fusion.171) | copy-start | bytes 196612
  304.0 7.2 %copy-start.36 = (f32[1,128,128]{2,1,0:T(8,128)S(1)}, f32[1,128,128]{2,1,0:T(8,128)}, u32[]{:S(2)}) copy-start(f32[1,128,128]{2,1,0:T(8,128)} %fusion.174) | copy-start | bytes 196612
  304.0 7.2 %copy-start.31 = (f32[1,128,128]{2,1,0:T(8,128)S(1)}, f32[1,128,128]{2,1,0:T(8,128)}, u32[]{:S(2)}) copy-start(f32[1,128,128]{2,1,0:T(8,128)} %fusion.180) | copy-start | bytes 196612
  304.0 7.2 %copy-start.34 = (f32[1,128,128]{2,1,0:T(8,128)S(1)}, f32[1,128,128]{2,1,0:T(8,128)}, u32[]{:S(2)}) copy-start(f32[1,128,128]{2,1,0:T(8,128)} %fusion.177) | copy-start | bytes 196612
  304.0 7.2 %copy-start.35 = (f32[1,128,128]{2,1,0:T(8,128)S(1)}, f32[1,128,128]{2,1,0:T(8,128)}, u32[]{:S(2)}) copy-start(f32[1,128,128]{2,1,0:T(8,128)} %fusion.185) | copy-start | bytes 196612
  311.2 1.8 copy-start.5
  318.7 3.2 copy-start.12
Sparse Core Ops, SparseCore 0:
  312.3 137.4 all-reduce.2
where the time goes:
time: 470 us; the launch traced here: 461 us
  waiting for transfers between devices  124 us (26%)
  local copies, waits for them, and re-layouts  95.3 us (20%)
  blocking collectives  86.6 us (18%)
  matrix products  60.8 us (13%)
  starting transfers between devices  41.8 us (9%)
  other arithmetic  36.5 us (8%)
  between operations  15.6 us (3%)
    psum x1, waiting for transfers between devices, body(): dw1 = lax.psum(_wgrad(xp, da), ('h', 'w'))  124 us
    psum x1, blocking collectives, body(): s = lax.psum(s.reshape(2, nb, GROUPS, cg).sum(-1), ('h', 'w')) / cnt  44.6 us
    psum x1, blocking collectives, body(): lax.psum(jnp.stack([(dn * xhatv).sum((1, 2)), dn.sum((1, 2))]), ('h', 'w'))  41.9 us
    unnamed x107, local copies, waits for them, and re-layouts  31.6 us
    dot_general x18, matrix products, _wgrad(): jnp.einsum('bhwc,bhwo->co', up[:, a:a + th, b:b + tw], v, preferred_eleme...  31.4 us
    ppermute x8, starting transfers between devices, _edge(): prev = lax.ppermute(hi, name, [(i, i + 1) for i in range(n - 1)])  30.9 us
    conv_general_dilated x14, local copies, waits for them, and re-layouts, _conv(): lax.conv_general_dilated(up, w, (1, 1), 'VALID', dimension_numbers=DN, pr...  30.5 us
    conv_general_dilated x4, matrix products, _conv(): lax.conv_general_dilated(up, w, (1, 1), 'VALID', dimension_numbers=DN, pr...  29.4 us
  transfers between devices with their start and end apart: 17, of which 1 were waited for; matrix products, arithmetic and copies ran while one was open for 20% of the time, Pallas kernels for 0%

commit v1 on v0

v1 whole, which is shorter than its diff:
```python
import functools

import jax
import jax.numpy as jnp
from jax import lax
from jax.experimental import pallas as pl
from jax.experimental.pallas import tpu as pltpu
from jax.sharding import PartitionSpec as P

MESH = pl.DeviceIdType.MESH
GROUPS = 32
EPS = 1e-5
RB, TB, NT, SL = 64, 16, 9, 8
C = 128
BF = jnp.bfloat16
F32 = jnp.float32
GC = 0.7978845608028654
GC2 = GC * 0.044715
DIRS = ((-1, 0), (1, 0), (0, -1), (0, 1), (-1, -1), (-1, 1), (1, -1), (1, 1))
OPP = (1, 0, 3, 2, 7, 6, 5, 4)


def _group_sum(v):
    lane = lax.broadcasted_iota(jnp.int32, v.shape, 1)
    v = v + jnp.where(lane % 2 == 0, pltpu.roll(v, C - 1, 1), pltpu.roll(v, 1, 1))
    return v + jnp.where(lane % 4 < 2, pltpu.roll(v, C - 2, 1), pltpu.roll(v, 2, 1))


def _fold(v):
    return v.reshape(v.shape[0] // SL, SL, C).sum(0)


def _kernel(nh, nw, th, tw, x_hbm, g_hbm, w1_hbm, w2_hbm, gam_ref, bet_ref,
            y_hbm, dx_hbm, dw1_hbm, dw2_hbm, dgam_ref, dbet_ref,
            xv, gv, w1v, w2v, wc1, wt1, wc2, wt2, ucat, gcat, zcat, gt, dat, av, dn, row, yv,
            hr, hc, hk, hrd, hcd, hkd, ec,
            st, sbuf, tt, tbuf, wacc, dwl, rd, rxy, zb, ag,
            ld, hs, hv, ss, sr, rs, rr, ysem):
    w = lax.axis_index('w')
    h = lax.axis_index('h')
    ndev = nh * nw
    me = w * nh + h
    cnt = float(th * nh * tw * nw * (C // GROUPS))

    barrier = pltpu.get_barrier_semaphore()

    @pl.loop(1, ndev)
    def _(k):
        d = lax.rem(me + k, ndev)
        pl.semaphore_signal(barrier, inc=1, device_id=(d // nh, d % nh), device_id_type=MESH)

    loads = [pltpu.make_async_copy(s, d, ld.at[i]) for i, (s, d) in enumerate(
        ((x_hbm, xv), (w1_hbm, w1v), (g_hbm, gv), (w2_hbm, w2v)))]
    for c in loads:
        c.start()

    def neighbour(d):
        dy, dx = DIRS[d]
        hh, ww = h + dy, w + dx
        ok = (hh >= 0) & (hh < nh) & (ww >= 0) & (ww < nw)
        return ok, (ww, hh)

    def halo(t, rows, cols, hrow, hcol, hcor, start):
        for d, (dy, dx) in enumerate(DIRS):
            ok, dev = neighbour(d)
            o = OPP[d]
            r = 0 if dy < 0 else th - 1
            if dx == 0:
                src, dst = rows.at[r], hrow.at[o]
            elif dy == 0:
                src, dst = cols.at[d - 2], hcol.at[o - 2]
            else:
                src, dst = rows.at[r, pl.ds(0 if dx < 0 else tw - TB, TB)], hcor.at[o - 4]
            cp = pltpu.make_async_remote_copy(src, dst, hs.at[t, d], hv.at[t, o], device_id=dev, device_id_type=MESH)
            if start:
                pl.when(ok)(cp.start)
            else:
                back = pltpu.make_async_remote_copy(
                    src, (hrow.at[d] if dx == 0 else hcol.at[d - 2] if dy == 0 else hcor.at[d - 4]),
                    hs.at[t, d], hv.at[t, d], device_id=dev, device_id_type=MESH)

                @pl.when(ok)
                def _():
                    back.wait_send()
                    back.wait_recv()

    def oks():
        return [neighbour(d)[0] for d in range(SL)]

    def cat_row(cat, r):
        for j in range(0, tw, RB):
            for b in range(3):
                cat[r, pl.ds(j, RB), pl.ds(b * C, C)] = row[pl.ds(7 + b + j, RB), :].astype(BF)

    def set_ends(left, right):
        row[7:SL, :] = left
        row[tw + SL:tw + NT, :] = right

    def patch(cat, r, left, right):
        it = lax.broadcasted_iota(jnp.int32, (TB, C), 0)
        a = cat[r, 0:TB, 0:C].astype(F32)
        cat[r, 0:TB, 0:C] = jnp.where(it == 0, left, a).astype(BF)
        b = cat[r, tw - TB:tw, 2 * C:3 * C].astype(F32)
        cat[r, tw - TB:tw, 2 * C:3 * C] = jnp.where(it == 15, right, b).astype(BF)

    def halo_rows(cat, okl, f, hrow, hcol, hcor):
        for e, r in ((0, 0), (1, th + 1)):
            for j in range(0, tw, RB):
                row[pl.ds(SL + j, RB), :] = jnp.where(okl[e], f([b[e, pl.ds(j, RB), :].astype(F32) for b in hrow]), 0.0)
            kl, kr = 2 * e, 2 * e + 1
            cl = f([b[kl].astype(F32) for b in hcor])
            cr = f([b[kr].astype(F32) for b in hcor])
            set_ends(jnp.where(okl[4 + kl], cl[15:TB, :], 0.0), jnp.where(okl[4 + kr], cr[0:1, :], 0.0))
            cat_row(cat, r)

        @pl.loop(0, th // SL)
        def _(k):
            r8 = pl.multiple_of(k * SL, SL)
            lf = jnp.where(okl[2], f([b[0, pl.ds(r8, SL), :].astype(F32) for b in hcol]), 0.0)
            rg = jnp.where(okl[3], f([b[1, pl.ds(r8, SL), :].astype(F32) for b in hcol]), 0.0)
            for i in range(SL):
                patch(cat, r8 + i + 1, lf[i:i + 1, :], rg[i:i + 1, :])

    def build(src, cat, t, vt):
        @pl.loop(0, th)
        def _(r):
            for j in range(0, tw, RB):
                row[pl.ds(SL + j, RB), :] = src[r, pl.ds(j, RB), :].astype(F32)
            ec[t, 0, pl.ds(r, 1), :] = row[SL:NT, :]
            ec[t, 1, pl.ds(r, 1), :] = row[tw + 7:tw + SL, :]
            cat_row(cat, r + 1)
            if vt is not None:
                vt[r + 1] = src[r].T

    def weights(wv, wc, wt):
        for r in range(4):
            for b in range(3):
                for t in range(2):
                    a = r - t
                    sl = (pl.ds((r * 3 + b) * C, C), pl.ds(t * C, C))
                    if 0 <= a < 3:
                        wc[sl] = wv[a * 3 + b]
                        wt[sl] = wv[(2 - a) * 3 + 2 - b].T
                    else:
                        wc[sl] = jnp.zeros((C, C), BF)
                        wt[sl] = jnp.zeros((C, C), BF)

    def conv(cat, wc, lo, hi, carry, fn):
        def step(q, carry):
            lhs = jnp.concatenate([
                jnp.concatenate([cat[4 * q + 2 * p + r] for r in range(4)], axis=1) for p in range(2)], axis=0)
            o = jnp.dot(lhs, wc[...], preferred_element_type=F32)
            return fn(q, o, carry)
        return lax.fori_loop(lo, hi, step, carry)

    def rows_of(o):
        return [o[(i // 2) * tw:(i // 2 + 1) * tw, (i % 2) * C:(i % 2 + 1) * C] for i in range(4)]

    def wgrad(vt, cat, dst):
        zero = jnp.zeros((C, tw), BF)
        vt[0] = zero
        vt[th + 1] = zero
        wacc[...] = jnp.zeros_like(wacc)
        wacc[0:C, :] = jnp.dot(vt[1], cat[0], preferred_element_type=F32)
        wacc[2 * C:3 * C, :] = jnp.dot(vt[th], cat[th + 1], preferred_element_type=F32)

        @pl.loop(0, th // 4)
        def _(q):
            lhs = jnp.concatenate([
                jnp.concatenate([vt[4 * q + s + 2 - a] for a in range(3)], axis=0) for s in range(4)], axis=1)
            rhs = cat[pl.ds(4 * q + 1, 4)].reshape(4 * tw, 3 * C)
            wacc[...] += jnp.dot(lhs, rhs, preferred_element_type=F32)

        for a in range(3):
            for b in range(3):
                dst[pl.ds((a * 3 + b) * C, C), :] = wacc[a * C:(a + 1) * C, b * C:(b + 1) * C].T

    def spread(src, buf, i):
        buf[me] = src[...]

        @pl.loop(1, ndev)
        def _(k):
            d = lax.rem(me + k, ndev)
            pltpu.make_async_remote_copy(src, buf.at[me], ss.at[i], sr.at[i], device_id=(d // nh, d % nh),
                                         device_id_type=MESH).start()

    def gather(buf, i):
        part = buf.at[pl.ds(0, ndev - 1)]
        pltpu.make_async_copy(part, part, sr.at[i]).wait()
        pltpu.make_async_copy(part, part, ss.at[i]).wait()
        s = buf[0]
        for k in range(1, ndev):
            s = s + buf[k]
        return s

    core, q_me = h % 2, h // 2
    half, piece = NT * C // 2, NT * C // SL

    def rcopy(src, dst, i, k, dev):
        return pltpu.make_async_remote_copy(src, dst, rs.at[i, k], rr.at[i, k], device_id=dev, device_id_type=MESH)

    def at(ref, i, start, n):
        return ref.at[i, pl.ds(pl.multiple_of(start, TB), n)]

    def ar_pair(i):
        other = 1 - core
        return rcopy(at(dwl, i, other * half, half), rd.at[i], i, 0, (w, h + 1 - 2 * core))

    def ar_xy(i):
        cps = []
        for k in range(1, 4):
            qo = q_me ^ k
            cps.append(rcopy(at(dwl, i, core * half + qo * piece, piece), rxy.at[i, k - 1], i, k, (w, qo * 2 + core)))
        return cps

    def ar_z(i):
        return [rcopy(zb.at[i, w], zb.at[i, w], i, 3 + k, (lax.rem(w + k, nw), h)) for k in range(1, nw)]

    def ar_z_in(i):
        return [rcopy(zb.at[i, w], zb.at[i, lax.rem(w + nw - k, nw)], i, 3 + k, (w, h)) for k in range(1, nw)]

    def ar_xy2(i):
        mine = at(ag, i, core * half + q_me * piece, piece)
        return [rcopy(mine, mine, i, 6 + k, (w, (q_me ^ k) * 2 + core)) for k in range(1, 4)]

    def ar_xy2_in(i):
        mine = at(ag, i, core * half + q_me * piece, piece)
        return [rcopy(mine, at(ag, i, core * half + (q_me ^ k) * piece, piece), i, 6 + k, (w, h)) for k in range(1, 4)]

    def ar_pair2(i):
        mine = at(ag, i, core * half, half)
        return rcopy(mine, mine, i, 10, (w, h + 1 - 2 * core))

    def ar_pair2_in(i):
        mine = at(ag, i, core * half, half)
        return rcopy(mine, at(ag, i, (1 - core) * half, half), i, 10, (w, h))

    outs = (dw1_hbm, dw2_hbm)

    def out_copy(i, c, k):
        s = pl.ds(pl.multiple_of(c * half, TB), half)
        return pltpu.make_async_copy(ag.at[i, s], outs[i].at[s], ysem.at[2 + 2 * i + k])

    def ar_step(i, n):
        if n == 0:
            ar_pair(i).start()
        elif n == 1:
            ar_pair(i).wait()
            for k in range(4):
                s = pl.ds(pl.multiple_of(core * half + k * piece, TB), piece)
                dwl[i, s, :] = dwl[i, s, :] + rd[i, pl.ds(k * piece, piece), :]
            for c in ar_xy(i):
                c.start()
        elif n == 2:
            for c in ar_xy(i):
                c.wait()
            s = pl.ds(pl.multiple_of(core * half + q_me * piece, TB), piece)
            zb[i, w] = dwl[i, s, :] + rxy[i, 0] + rxy[i, 1] + rxy[i, 2]
            for c in ar_z(i):
                c.start()
        elif n == 3:
            for c in ar_z(i):
                c.wait_send()
            for c in ar_z_in(i):
                c.wait_recv()
            s = zb[i, 0]
            for k in range(1, nw):
                s = s + zb[i, k]
            ag[i, pl.ds(pl.multiple_of(core * half + q_me * piece, TB), piece), :] = s
            for c in ar_xy2(i):
                c.start()
        elif n == 4:
            for c in ar_xy2(i):
                c.wait_send()
            for c in ar_xy2_in(i):
                c.wait_recv()
            ar_pair2(i).start()
            out_copy(i, core, 0).start()
        else:
            ar_pair2(i).wait_send()
            ar_pair2_in(i).wait_recv()
            out_copy(i, 1 - core, 1).start()

    okl = oks()
    loads[0].wait()
    build(xv, ucat, 0, None)
    loads[1].wait()
    weights(w1v, wc1, wt1)
    pl.semaphore_wait(barrier, ndev - 1)
    halo(0, xv, ec.at[0], hr.at[0], hc.at[0], hk.at[0], True)
    loads[2].wait()
    build(gv, gcat, 1, gt)
    halo(1, gv, ec.at[1], hr.at[1], hc.at[1], hk.at[1], True)
    loads[3].wait()
    weights(w2v, wc2, wt2)
    halo(0, xv, ec.at[0], hr.at[0], hc.at[0], hk.at[0], False)
    halo_rows(ucat, okl, lambda v: v[0], [hr.at[0]], [hc.at[0]], [hk.at[0]])

    def fin_a(q, o, carry):
        s1, s2 = carry
        for i, v in enumerate(rows_of(o)):
            vb = v.astype(BF)
            av[4 * q + i] = vb
            vf = vb.astype(F32)
            ec[2, 0, pl.ds(4 * q + i, 1), :] = vf[0:1, :]
            ec[2, 1, pl.ds(4 * q + i, 1), :] = vf[tw - 1:tw, :]
            s1 = s1 + _fold(vf)
            s2 = s2 + _fold(vf * vf)
        return s1, s2

    z8 = jnp.zeros((SL, C), F32)
    s1, s2 = conv(ucat, wc1, 0, th // 4, (z8, z8), fin_a)
    st[0:1, :] = s1.sum(0, keepdims=True)
    st[1:2, :] = s2.sum(0, keepdims=True)
    spread(st, sbuf, 0)
    halo(2, av, ec.at[2], hr.at[2], hc.at[2], hk.at[2], True)

    halo(1, gv, ec.at[1], hr.at[1], hc.at[1], hk.at[1], False)
    halo_rows(gcat, okl, lambda v: v[0], [hr.at[1]], [hc.at[1]], [hk.at[1]])

    def fin_dz(q, o, carry):
        for i, v in enumerate(rows_of(o)):
            dn[4 * q + i] = v
        return carry

    conv(gcat, wt2, 0, th // 4, 0, fin_dz)

    tot = _group_sum(gather(sbuf, 0)) / cnt
    mean = tot[0:1, :]
    rstd = lax.rsqrt(tot[1:2, :] - mean * mean + EPS)
    sh = -mean * rstd
    gam = gam_ref[...]
    bet = bet_ref[...]

    def act(a):
        xh = a * rstd + sh
        n = xh * gam + bet
        n2 = n * n
        p = 0.5 + 0.5 * jnp.tanh(n * (GC + GC2 * n2))
        return xh, n2, p, n * p

    def zrow(r, carry):
        t0, t1 = carry
        for j in range(0, tw, RB):
            s = pl.ds(j, RB)
            xh, n2, p, z = act(av[r, s, :].astype(F32))
            row[pl.ds(SL + j, RB), :] = z
            d = dn[r, s, :] * (p + z * (1.0 - p) * (2.0 * GC + 6.0 * GC2 * n2))
            dn[r, s, :] = d
            if j == 0:
                ec[3, 0, pl.ds(r, 1), :] = d[0:1, :]
            if j + RB == tw:
                ec[3, 1, pl.ds(r, 1), :] = d[63:RB, :]
            t0 = t0 + _fold(d * xh)
            t1 = t1 + _fold(d)
        cat_row(zcat, r + 1)
        return t0, t1

    t0, t1 = lax.fori_loop(0, th, zrow, (z8, z8))
    tt[0:1, :] = t0.sum(0, keepdims=True)
    tt[1:2, :] = t1.sum(0, keepdims=True)
    spread(tt, tbuf, 1)
    halo(3, dn, ec.at[3], hrd, hcd, hkd, True)

    halo(2, av, ec.at[2], hr.at[2], hc.at[2], hk.at[2], False)
    halo_rows(zcat, okl, lambda v: act(v[0])[3], [hr.at[2]], [hc.at[2]], [hk.at[2]])

    wgrad(gt, zcat, dwl.at[1])
    ar_step(1, 0)

    t = gather(tbuf, 1)
    dgam_ref[...] = t[0:1, :]
    dbet_ref[...] = t[1:2, :]
    u = _group_sum(t * gam) / cnt
    k1 = gam * rstd
    k2 = -rstd * rstd * u[0:1, :]
    k3 = -rstd * (u[1:2, :] + sh * u[0:1, :])

    @pl.loop(0, th)
    def _(r):
        for j in range(0, tw, RB):
            s = pl.ds(j, RB)
            v = dn[r, s, :] * k1 + av[r, s, :].astype(F32) * k2 + k3
            row[pl.ds(SL + j, RB), :] = v
        cat_row(gcat, r + 1)
        dat[r + 1] = gcat[r + 1, :, C:2 * C].T

    halo(3, dn, ec.at[3], hrd, hcd, hkd, False)
    halo_rows(gcat, okl, lambda v: v[0] * k1 + v[1] * k2 + k3, [hrd, hr.at[2]], [hcd, hc.at[2]], [hkd, hk.at[2]])
    ar_step(1, 1)

    wgrad(dat, ucat, dwl.at[0])
    ar_step(0, 0)
    ar_step(1, 2)

    def ycopy(k, q):
        s = pl.ds(4 * q, 4)
        return pltpu.make_async_copy(yv.at[k, s], (dx_hbm, y_hbm)[k].at[s], ysem.at[k])

    def fin_dx(q, o, carry):
        for i, v in enumerate(rows_of(o)):
            yv[0, 4 * q + i] = (v + gv[4 * q + i].astype(F32)).astype(BF)
        ycopy(0, q).start()
        return carry

    def fin_y(q, o, carry):
        for i, v in enumerate(rows_of(o)):
            yv[1, 4 * q + i] = (v + xv[4 * q + i].astype(F32)).astype(BF)
        ycopy(1, q).start()
        return carry

    n4 = th // 4
    conv(gcat, wt1, 0, n4 // 2, 0, fin_dx)
    ar_step(0, 1)
    ar_step(1, 3)
    conv(gcat, wt1, n4 // 2, n4, 0, fin_dx)
    ar_step(0, 2)
    ar_step(1, 4)
    conv(zcat, wc2, 0, n4, 0, fin_y)
    ar_step(0, 3)
    ar_step(1, 5)
    ar_step(0, 4)
    pltpu.make_async_copy(yv.at[0], dx_hbm, ysem.at[0]).wait()
    pltpu.make_async_copy(yv.at[1], y_hbm, ysem.at[1]).wait()
    ar_step(0, 5)
    for i in range(2):
        out_copy(i, core, 0).wait()
        out_copy(i, 1 - core, 1).wait()


def solution(mesh):
    nh, nw = mesh.shape['h'], mesh.shape['w']
    tile = P(None, 'h', 'w', None)

    def body(x, w1, gamma, beta, w2, g):
        _, th, tw, c = x.shape
        anys = pl.BlockSpec(memory_space=pl.ANY)
        vm = pl.BlockSpec(memory_space=pltpu.VMEM)
        V = pltpu.VMEM
        D = pltpu.SemaphoreType.DMA
        img = jax.ShapeDtypeStruct((th, tw, c), BF)
        wsh = jax.ShapeDtypeStruct((NT * c, c), F32)
        vec = jax.ShapeDtypeStruct((1, c), F32)
        cat = V((th + 2, tw, 3 * c), BF)
        ndev = nh * nw
        scratch = dict(
            xv=V((th, tw, c), BF), gv=V((th, tw, c), BF), w1v=V((NT, c, c), BF), w2v=V((NT, c, c), BF),
            wc1=V((12 * c, 2 * c), BF), wt1=V((12 * c, 2 * c), BF), wc2=V((12 * c, 2 * c), BF), wt2=V((12 * c, 2 * c), BF),
            ucat=cat, gcat=cat, zcat=cat, gt=V((th + 2, c, tw), BF), dat=V((th + 2, c, tw), BF),
            av=V((th, tw, c), BF), dn=V((th, tw, c), F32), row=V((tw + TB, c), F32), yv=V((2, th, tw, c), BF),
            hr=V((3, 2, tw, c), BF), hc=V((3, 2, th, c), F32), hk=V((3, 4, TB, c), BF),
            hrd=V((2, tw, c), F32), hcd=V((2, th, c), F32), hkd=V((4, TB, c), F32), ec=V((4, 2, th, c), F32),
            st=V((2, c), F32), sbuf=V((ndev, 2, c), F32), tt=V((2, c), F32), tbuf=V((ndev, 2, c), F32),
            wacc=V((3 * c, 3 * c), F32), dwl=V((2, NT * c, c), F32), rd=V((2, NT * c // 2, c), F32),
            rxy=V((2, 3, NT * c // SL, c), F32), zb=V((2, nw, NT * c // SL, c), F32), ag=V((2, NT * c, c), F32),
            ld=D((4,)), hs=D((4, SL)), hv=D((4, SL)), ss=D((2,)), sr=D((2,)), rs=D((2, 11)), rr=D((2, 11)), ysem=D((6,)),
        )
        y, dx, dw1, dw2, dg, db = pl.pallas_call(
            functools.partial(_kernel, nh, nw, th, tw),
            out_shape=(img, img, wsh, wsh, vec, vec),
            in_specs=[anys] * 4 + [vm] * 2,
            out_specs=(anys,) * 4 + (vm,) * 2,
            scratch_shapes=list(scratch.values()),
            compiler_params=pltpu.CompilerParams(collective_id=0, has_side_effects=True, vmem_limit_bytes=62 << 20),
        )(x.reshape(th, tw, c), g.reshape(th, tw, c), w1.reshape(NT, c, c), w2.reshape(NT, c, c),
          gamma.reshape(1, c), beta.reshape(1, c))
        return (y.reshape(x.shape), dx.reshape(x.shape), dw1.reshape(3, 3, c, c), dw2.reshape(3, 3, c, c),
                dg.reshape(c), db.reshape(c))

    return jax.shard_map(body, mesh=mesh, in_specs=(tile, P(), P(), P(), P(), tile),
                         out_specs=(tile, tile, P(), P(), P(), P()), check_vma=False)
```

time: 470 us -> 73.9 us (0.16); the launches traced: 461 us -> 73.5 us
  waiting for transfers between devices: 124 us -> 0 us
  local copies, waits for them, and re-layouts: 95.3 us -> 7.39 us
  blocking collectives: 86.6 us -> 0 us
  Pallas kernels: 0 us -> 65.5 us
  matrix products: 60.8 us -> 0 us
  starting transfers between devices: 41.8 us -> 0 us
  other arithmetic: 36.5 us -> 0 us
  between operations: 15.6 us -> 0.66 us
    psum x1 -> x0, waiting for transfers between devices: 124 us -> none  [body(): dw1 = lax.psum(_wgrad(xp, da), ('h', 'w'))]
    psum x2 -> x0, blocking collectives: 86.6 us -> none  [the longest x1 44.6 us: body(): s = lax.psum(s.reshape(2, nb, GROUPS, cg).sum(-1), ('h', 'w')) / cnt]
    pallas_call x0 -> x1, Pallas kernels: none -> 65.5 us  [body(): pl.pallas_call(functools.partial(_kernel, nh, nw, th, tw), out_shape=(img...]
    ppermute x16 -> x0, starting transfers between devices: 41.7 us -> none  [the longest x8 30.9 us: _edge(): prev = lax.ppermute(hi, name, [(i, i + 1) for i in range(n - 1)])]
    dot_general x18 -> x0, matrix products: 31.4 us -> none  [_wgrad(): jnp.einsum('bhwc,bhwo->co', up[:, a:a + th, b:b + tw], v, preferred_eleme...]
    conv_general_dilated x14 -> x0, local copies, waits for them, and re-layouts: 30.5 us -> none  [_conv(): lax.conv_general_dilated(up, w, (1, 1), 'VALID', dimension_numbers=DN, pr...]
    conv_general_dilated x4 -> x0, matrix products: 29.4 us -> none  [_conv(): lax.conv_general_dilated(up, w, (1, 1), 'VALID', dimension_numbers=DN, pr...]
    unnamed x107 -> x16, local copies, waits for them, and re-layouts: 31.6 us -> 7.39 us
  transfers between devices with their start and end apart: 17 -> 0, of which waited for: 1 -> 0; matrix products, arithmetic and copies ran while one was open for 20% -> 0% of each run, Pallas kernels for 0% -> 0%
where the time goes in v1:
time: 73.9 us; the launch traced here: 73.5 us
  Pallas kernels  65.5 us (89%)
  local copies, waits for them, and re-layouts  7.39 us (10%)
    pallas_call x1, Pallas kernels, body(): pl.pallas_call(functools.partial(_kernel, nh, nw, th, tw), out_shape=(img...  65.5 us
    unnamed x16, local copies, waits for them, and re-layouts  7.39 us

profile of v1, /device:TPU:0, one launch (start us, length us, event | category | flops | bytes accessed | tf_op | source)
XLA Modules:
  0.0 73.5 jit_solution(5051744426015426320)
XLA Ops:
  0.6 65.5 %shard_map.109 = (bf16[32,256,128]{2,1,0:T(8,128)(2,1)}, bf16[32,256,128]{2,1,0:T(8,128)(2,1)}, f32[1152,128]{1,0:T(8,128)}, f32[1152,128]{1,0:T(8,128)}, f32[1,128]{1,0:T(1,128)}, /*index=5*/f32[1,128]{1,0:T(1,128)}) custom-call(bf16[32,256,128]{2,1,0:T(8,128)(2,1)} %bitcast.14, bf16[32,256,128]{2,1,0:T(8,128)(2,1)} %bitcast.15, ...), custom_call_target="tpu_custom_call" | custom-call | tf_op jit(solution)/shard_map/pallas_call | solution.py:458
  66.1 0.0 copy-start
  66.1 3.3 %copy.18 = bf16[1,32,256,128]{3,2,1,0:T(8,128)(2,1)} copy(bf16[1,32,256,128]{3,2,1,0:T(8,128)(2,1)} %bitcast.13) | data formatting | bytes 4194304
  69.4 0.0 copy-done
  69.4 0.0 copy-start.2
  69.4 0.0 copy-start.1
  69.4 1.3 %copy.19 = bf16[1,32,256,128]{3,2,1,0:T(8,128)(2,1)} copy(bf16[1,32,256,128]{3,2,1,0:T(8,128)(2,1)S(1)} %bitcast.12) | data formatting | bytes 4194304
  70.7 0.1 copy-done.2
  70.9 0.0 copy-start.4
  70.9 0.0 copy-start.3
  70.9 0.8 %copy.20 = f32[3,3,128,128]{3,2,1,0:T(8,128)} copy(f32[3,3,128,128]{3,2,1,0:T(8,128)S(1)} %bitcast.17) | data formatting | bytes 1179648
  71.7 0.0 copy-done.1
  71.7 0.8 %copy.21 = f32[3,3,128,128]{3,2,1,0:T(8,128)} copy(f32[3,3,128,128]{3,2,1,0:T(8,128)S(1)} %bitcast.16) | data formatting | bytes 1179648
  72.5 0.0 copy-done.4
  72.5 0.5 copy.22
  73.0 0.0 copy-done.3
  73.0 0.5 copy.23
Async XLA Ops:
  66.1 3.3 %copy-start = (bf16[32,256,128]{2,1,0:T(8,128)(2,1)S(1)}, bf16[32,256,128]{2,1,0:T(8,128)(2,1)}, u32[]{:S(2)}) copy-start(bf16[32,256,128]{2,1,0:T(8,128)(2,1)} %get-tuple-element.13) | copy-start | bytes 6291460
  69.4 1.4 %copy-start.2 = (f32[1152,128]{1,0:T(8,128)S(1)}, f32[1152,128]{1,0:T(8,128)}, u32[]{:S(2)}) copy-start(f32[1152,128]{1,0:T(8,128)} %get-tuple-element.14) | copy-start | bytes 1769476
  69.4 2.3 %copy-start.1 = (f32[1152,128]{1,0:T(8,128)S(1)}, f32[1152,128]{1,0:T(8,128)}, u32[]{:S(2)}) copy-start(f32[1152,128]{1,0:T(8,128)} %get-tuple-element.15) | copy-start | bytes 1769476
  70.9 1.6 %copy-start.4 = (f32[1,128]{1,0:T(1,128)S(1)}, f32[1,128]{1,0:T(1,128)}, u32[]{:S(2)}) copy-start(f32[1,128]{1,0:T(1,128)} %get-tuple-element.16) | copy-start | bytes 1540
  70.9 2.2 %copy-start.3 = (f32[1,128]{1,0:T(1,128)S(1)}, f32[1,128]{1,0:T(1,128)}, u32[]{:S(2)}) copy-start(f32[1,128]{1,0:T(1,128)} %get-tuple-element.17) | copy-start | bytes 1540

commit v2 on v1

--- a/solution.py
+++ b/solution.py
@@ -30,12 +30,12 @@
     return v.reshape(v.shape[0] // SL, SL, C).sum(0)
 
 
-def _kernel(nh, nw, th, tw, x_hbm, g_hbm, w1_hbm, w2_hbm, gam_ref, bet_ref,
-            y_hbm, dx_hbm, dw1_hbm, dw2_hbm, dgam_ref, dbet_ref,
-            xv, gv, w1v, w2v, wc1, wt1, wc2, wt2, ucat, gcat, zcat, gt, dat, av, dn, row, yv,
+def _kernel(nh, nw, th, tw, x_hbm, g_hbm, w1v, w2v, gam_ref, bet_ref,
+            y_ref, dx_ref, dw1_ref, dw2_ref, dgam_ref, dbet_ref,
+            xv, gv, wc1, wt1, wc2, wt2, ucat, gcat, zcat, gt, dat, av, dn, row,
             hr, hc, hk, hrd, hcd, hkd, ec,
-            st, sbuf, tt, tbuf, wacc, dwl, rd, rxy, zb, ag,
-            ld, hs, hv, ss, sr, rs, rr, ysem):
+            st, sbuf, tt, tbuf, wacc, dwl, rd, rxy, zb,
+            ld, hs, hv, ss, sr, rs, rr):
     w = lax.axis_index('w')
     h = lax.axis_index('h')
     ndev = nh * nw
@@ -50,7 +50,7 @@
         pl.semaphore_signal(barrier, inc=1, device_id=(d // nh, d % nh), device_id_type=MESH)
 
     loads = [pltpu.make_async_copy(s, d, ld.at[i]) for i, (s, d) in enumerate(
-        ((x_hbm, xv), (w1_hbm, w1v), (g_hbm, gv), (w2_hbm, w2v)))]
+        ((x_hbm, xv), (g_hbm, gv)))]
     for c in loads:
         c.start()
 
@@ -199,18 +199,20 @@
     def rcopy(src, dst, i, k, dev):
         return pltpu.make_async_remote_copy(src, dst, rs.at[i, k], rr.at[i, k], device_id=dev, device_id_type=MESH)
 
-    def at(ref, i, start, n):
-        return ref.at[i, pl.ds(pl.multiple_of(start, TB), n)]
+    outs = (dw1_ref, dw2_ref)
+
+    def at(ref, start, n):
+        return ref.at[pl.ds(pl.multiple_of(start, TB), n)]
 
     def ar_pair(i):
         other = 1 - core
-        return rcopy(at(dwl, i, other * half, half), rd.at[i], i, 0, (w, h + 1 - 2 * core))
+        return rcopy(at(dwl.at[i], other * half, half), rd.at[i], i, 0, (w, h + 1 - 2 * core))
 
     def ar_xy(i):
         cps = []
         for k in range(1, 4):
             qo = q_me ^ k
-            cps.append(rcopy(at(dwl, i, core * half + qo * piece, piece), rxy.at[i, k - 1], i, k, (w, qo * 2 + core)))
+            cps.append(rcopy(at(dwl.at[i], core * half + qo * piece, piece), rxy.at[i, k - 1], i, k, (w, qo * 2 + core)))
         return cps
 
     def ar_z(i):
@@ -220,26 +222,20 @@
         return [rcopy(zb.at[i, w], zb.at[i, lax.rem(w + nw - k, nw)], i, 3 + k, (w, h)) for k in range(1, nw)]
 
     def ar_xy2(i):
-        mine = at(ag, i, core * half + q_me * piece, piece)
+        mine = at(outs[i], core * half + q_me * piece, piece)
         return [rcopy(mine, mine, i, 6 + k, (w, (q_me ^ k) * 2 + core)) for k in range(1, 4)]
 
     def ar_xy2_in(i):
-        mine = at(ag, i, core * half + q_me * piece, piece)
-        return [rcopy(mine, at(ag, i, core * half + (q_me ^ k) * piece, piece), i, 6 + k, (w, h)) for k in range(1, 4)]
+        mine = at(outs[i], core * half + q_me * piece, piece)
+        return [rcopy(mine, at(outs[i], core * half + (q_me ^ k) * piece, piece), i, 6 + k, (w, h)) for k in range(1, 4)]
 
     def ar_pair2(i):
-        mine = at(ag, i, core * half, half)
+        mine = at(outs[i], core * half, half)
         return rcopy(mine, mine, i, 10, (w, h + 1 - 2 * core))
 
     def ar_pair2_in(i):
-        mine = at(ag, i, core * half, half)
-        return rcopy(mine, at(ag, i, (1 - core) * half, half), i, 10, (w, h))
-
-    outs = (dw1_hbm, dw2_hbm)
-
-    def out_copy(i, c, k):
-        s = pl.ds(pl.multiple_of(c * half, TB), half)
-        return pltpu.make_async_copy(ag.at[i, s], outs[i].at[s], ysem.at[2 + 2 * i + k])
+        mine = at(outs[i], core * half, half)
+        return rcopy(mine, at(outs[i], (1 - core) * half, half), i, 10, (w, h))
 
     def ar_step(i, n):
         if n == 0:
@@ -266,7 +262,7 @@
             s = zb[i, 0]
             for k in range(1, nw):
                 s = s + zb[i, k]
-            ag[i, pl.ds(pl.multiple_of(core * half + q_me * piece, TB), piece), :] = s
+            outs[i][pl.ds(pl.multiple_of(core * half + q_me * piece, TB), piece), :] = s
             for c in ar_xy2(i):
                 c.start()
         elif n == 4:
@@ -275,23 +271,19 @@
             for c in ar_xy2_in(i):
                 c.wait_recv()
             ar_pair2(i).start()
-            out_copy(i, core, 0).start()
         else:
             ar_pair2(i).wait_send()
             ar_pair2_in(i).wait_recv()
-            out_copy(i, 1 - core, 1).start()
 
     okl = oks()
     loads[0].wait()
     build(xv, ucat, 0, None)
-    loads[1].wait()
     weights(w1v, wc1, wt1)
     pl.semaphore_wait(barrier, ndev - 1)
     halo(0, xv, ec.at[0], hr.at[0], hc.at[0], hk.at[0], True)
-    loads[2].wait()
+    loads[1].wait()
     build(gv, gcat, 1, gt)
     halo(1, gv, ec.at[1], hr.at[1], hc.at[1], hk.at[1], True)
-    loads[3].wait()
     weights(w2v, wc2, wt2)
     halo(0, xv, ec.at[0], hr.at[0], hc.at[0], hk.at[0], False)
     halo_rows(ucat, okl, lambda v: v[0], [hr.at[0]], [hc.at[0]], [hk.at[0]])
@@ -393,20 +385,14 @@
     ar_step(0, 0)
     ar_step(1, 2)
 
-    def ycopy(k, q):
-        s = pl.ds(4 * q, 4)
-        return pltpu.make_async_copy(yv.at[k, s], (dx_hbm, y_hbm)[k].at[s], ysem.at[k])
-
     def fin_dx(q, o, carry):
         for i, v in enumerate(rows_of(o)):
-            yv[0, 4 * q + i] = (v + gv[4 * q + i].astype(F32)).astype(BF)
-        ycopy(0, q).start()
+            dx_ref[4 * q + i] = (v + gv[4 * q + i].astype(F32)).astype(BF)
         return carry
 
     def fin_y(q, o, carry):
         for i, v in enumerate(rows_of(o)):
-            yv[1, 4 * q + i] = (v + xv[4 * q + i].astype(F32)).astype(BF)
-        ycopy(1, q).start()
+            y_ref[4 * q + i] = (v + xv[4 * q + i].astype(F32)).astype(BF)
         return carry
 
     n4 = th // 4
@@ -420,12 +406,15 @@
     ar_step(0, 3)
     ar_step(1, 5)
     ar_step(0, 4)
-    pltpu.make_async_copy(yv.at[0], dx_hbm, ysem.at[0]).wait()
-    pltpu.make_async_copy(yv.at[1], y_hbm, ysem.at[1]).wait()
     ar_step(0, 5)
-    for i in range(2):
-        out_copy(i, core, 0).wait()
-        out_copy(i, 1 - core, 1).wait()
+
+
+def _flush(n, *refs):
+    cps = [pltpu.make_async_copy(refs[i], refs[n + i], refs[-1].at[i]) for i in range(n)]
+    for c in cps:
+        c.start()
+    for c in cps:
+        c.wait()
 
 
 def solution(mesh):
@@ -434,7 +423,7 @@
 
     def body(x, w1, gamma, beta, w2, g):
         _, th, tw, c = x.shape
-        anys = pl.BlockSpec(memory_space=pl.ANY)
+        hbm = pl.BlockSpec(memory_space=pltpu.HBM)
         vm = pl.BlockSpec(memory_space=pltpu.VMEM)
         V = pltpu.VMEM
         D = pltpu.SemaphoreType.DMA
@@ -444,26 +433,34 @@
         cat = V((th + 2, tw, 3 * c), BF)
         ndev = nh * nw
         scratch = dict(
-            xv=V((th, tw, c), BF), gv=V((th, tw, c), BF), w1v=V((NT, c, c), BF), w2v=V((NT, c, c), BF),
+            xv=V((th, tw, c), BF), gv=V((th, tw, c), BF),
             wc1=V((12 * c, 2 * c), BF), wt1=V((12 * c, 2 * c), BF), wc2=V((12 * c, 2 * c), BF), wt2=V((12 * c, 2 * c), BF),
             ucat=cat, gcat=cat, zcat=cat, gt=V((th + 2, c, tw), BF), dat=V((th + 2, c, tw), BF),
-            av=V((th, tw, c), BF), dn=V((th, tw, c), F32), row=V((tw + TB, c), F32), yv=V((2, th, tw, c), BF),
+            av=V((th, tw, c), BF), dn=V((th, tw, c), F32), row=V((tw + TB, c), F32),
             hr=V((3, 2, tw, c), BF), hc=V((3, 2, th, c), F32), hk=V((3, 4, TB, c), BF),
             hrd=V((2, tw, c), F32), hcd=V((2, th, c), F32), hkd=V((4, TB, c), F32), ec=V((4, 2, th, c), F32),
             st=V((2, c), F32), sbuf=V((ndev, 2, c), F32), tt=V((2, c), F32), tbuf=V((ndev, 2, c), F32),
             wacc=V((3 * c, 3 * c), F32), dwl=V((2, NT * c, c), F32), rd=V((2, NT * c // 2, c), F32),
-            rxy=V((2, 3, NT * c // SL, c), F32), zb=V((2, nw, NT * c // SL, c), F32), ag=V((2, NT * c, c), F32),
-            ld=D((4,)), hs=D((4, SL)), hv=D((4, SL)), ss=D((2,)), sr=D((2,)), rs=D((2, 11)), rr=D((2, 11)), ysem=D((6,)),
+            rxy=V((2, 3, NT * c // SL, c), F32), zb=V((2, nw, NT * c // SL, c), F32),
+            ld=D((2,)), hs=D((4, SL)), hv=D((4, SL)), ss=D((2,)), sr=D((2,)), rs=D((2, 11)), rr=D((2, 11)),
         )
-        y, dx, dw1, dw2, dg, db = pl.pallas_call(
+        res = pl.pallas_call(
             functools.partial(_kernel, nh, nw, th, tw),
             out_shape=(img, img, wsh, wsh, vec, vec),
-            in_specs=[anys] * 4 + [vm] * 2,
-            out_specs=(anys,) * 4 + (vm,) * 2,
+            in_specs=[hbm] * 2 + [vm] * 4,
+            out_specs=(vm,) * 6,
             scratch_shapes=list(scratch.values()),
-            compiler_params=pltpu.CompilerParams(collective_id=0, has_side_effects=True, vmem_limit_bytes=62 << 20),
+            compiler_params=pltpu.CompilerParams(collective_id=0, has_side_effects=True, vmem_limit_bytes=48 << 20),
         )(x.reshape(th, tw, c), g.reshape(th, tw, c), w1.reshape(NT, c, c), w2.reshape(NT, c, c),
           gamma.reshape(1, c), beta.reshape(1, c))
+        y, dx, dw1, dw2, dg, db = pl.pallas_call(
+            functools.partial(_flush, len(res)),
+            out_shape=(img, img, wsh, wsh, vec, vec),
+            in_specs=[vm] * len(res),
+            out_specs=(hbm,) * len(res),
+            scratch_shapes=[D((len(res),))],
+            compiler_params=pltpu.CompilerParams(vmem_limit_bytes=1 << 20),
+        )(*res)
         return (y.reshape(x.shape), dx.reshape(x.shape), dw1.reshape(3, 3, c, c), dw2.reshape(3, 3, c, c),
                 dg.reshape(c), db.reshape(c))
 

time: 73.9 us -> 70.2 us (0.950)
  local copies, waits for them, and re-layouts: 7.39 us -> 3.23 us
    unnamed x16 -> x8, local copies, waits for them, and re-layouts: 7.39 us -> 3.23 us
    pallas_call x0 -> x1, Pallas kernels: none -> 2.43 us  [body(): pl.pallas_call(functools.partial(_flush, len(res)), out_shape=(img, img,...]
    pallas_call x1, Pallas kernels: 65.5 us -> 63.5 us  [body(): pl.pallas_call(functools.partial(_kernel, nh, nw, th, tw), out_shape=(img...]
where the time goes in v2:
time: 70.2 us; the launch traced here: 69.8 us
  Pallas kernels  65.9 us (94%)
  local copies, waits for them, and re-layouts  3.23 us (5%)
    pallas_call x1, Pallas kernels, body(): pl.pallas_call(functools.partial(_kernel, nh, nw, th, tw), out_shape=(img...  63.5 us
    unnamed x8, local copies, waits for them, and re-layouts  3.23 us
    pallas_call x1, Pallas kernels, body(): pl.pallas_call(functools.partial(_flush, len(res)), out_shape=(img, img,...  2.43 us

profile of v2, /device:TPU:0, one launch (start us, length us, event | category | flops | bytes accessed | tf_op | source)
XLA Modules:
  0.0 69.8 jit_solution(12421267822892239347)
XLA Ops:
  0.6 0.0 copy-start
  0.6 1.0 %copy-done = bf16[3,3,128,128]{3,2,1,0:T(8,128)(2,1)S(1)} copy-done((bf16[3,3,128,128]{3,2,1,0:T(8,128)(2,1)S(1)}, bf16[3,3,128,128]{3,2,1,0:T(8,128)(2,1)}, u32[]{:S(2)}) %copy-start) | copy-done | bytes 294936
  1.6 0.0 copy-start.1
  1.6 1.0 %copy-done.1 = bf16[3,3,128,128]{3,2,1,0:T(8,128)(2,1)S(1)} copy-done((bf16[3,3,128,128]{3,2,1,0:T(8,128)(2,1)S(1)}, bf16[3,3,128,128]{3,2,1,0:T(8,128)(2,1)}, u32[]{:S(2)}) %copy-start.1) | copy-done | bytes 294936
  2.6 0.0 copy-start.2
  2.6 0.7 copy-done.2
  3.2 0.0 copy-start.3
  3.2 0.7 copy-done.3
  3.9 63.5 %shard_map.109 = (bf16[32,256,128]{2,1,0:T(8,128)(2,1)S(1)}, bf16[32,256,128]{2,1,0:T(8,128)(2,1)S(1)}, f32[1152,128]{1,0:T(8,128)S(1)}, f32[1152,128]{1,0:T(8,1...) custom-call(bf16[32,256,128]{2,1,0:T(8,128)(2,1)} %bitcast.16, bf16[32,256,128]{2,1,0:T(8,128)(2,1)} %bitcast.17, ...), custom_call_target="tpu_custom_call" | custom-call | tf_op jit(solution)/shard_map/pallas_call | solution.py:447
  67.3 2.4 %shard_map.110 = (bf16[32,256,128]{2,1,0:T(8,128)(2,1)}, bf16[32,256,128]{2,1,0:T(8,128)(2,1)}, f32[1152,128]{1,0:T(8,128)}, f32[1152,128]{1,0:T(8,128)}, f32[1,128]{1,0:T(1,128)}, /*index=5*/f32[1,128]{1,0:T(1,128)}) custom-call(bf16[32,256,128]{2,1,0:T(8,128)(2,1)S(1)} %get-tuple-element.18.refs_0_, bf16[32,256,128]{2,1,0:T(8,128)(2,1)S(1)} %get-tuple-element.19.refs_1_, ...), custom_call_target="tpu_custom_call" | custom-call | tf_op jit(solution)/shard_map/pallas_call | solution.py:456
Async XLA Ops:
  0.6 1.0 %copy-start = (bf16[3,3,128,128]{3,2,1,0:T(8,128)(2,1)S(1)}, bf16[3,3,128,128]{3,2,1,0:T(8,128)(2,1)}, u32[]{:S(2)}) copy-start(bf16[3,3,128,128]{3,2,1,0:T(8,128)(2,1)} %param.7) | copy-start | bytes 884740
  1.6 1.0 %copy-start.1 = (bf16[3,3,128,128]{3,2,1,0:T(8,128)(2,1)S(1)}, bf16[3,3,128,128]{3,2,1,0:T(8,128)(2,1)}, u32[]{:S(2)}) copy-start(bf16[3,3,128,128]{3,2,1,0:T(8,128)(2,1)} %param.10) | copy-start | bytes 884740
  2.6 0.7 copy-start.2
  3.2 0.7 copy-start.3

commit v3 on v2

v3 whole, which is shorter than its diff:
```python
import functools

import jax
import jax.numpy as jnp
from jax import lax
from jax.experimental import pallas as pl
from jax.experimental.pallas import tpu as pltpu
from jax.sharding import PartitionSpec as P

MESH = pl.DeviceIdType.MESH
GROUPS = 32
EPS = 1e-5
RB, TB, NT, SL = 64, 16, 9, 8
C = 128
C2, C3, ZERO = 2 * C, 3 * C, 0.0
BF = jnp.bfloat16
F32 = jnp.float32
GC = 0.7978845608028654
GC2 = GC * 0.044715
DIRS = ((-1, 0), (1, 0), (0, -1), (0, 1), (-1, -1), (-1, 1), (1, -1), (1, 1))
OPP = (1, 0, 3, 2, 7, 6, 5, 4)


def _group_sum(v):
    lane = lax.broadcasted_iota(jnp.int32, v.shape, 1)
    v = v + jnp.where(lane % 2 == 0, pltpu.roll(v, C - 1, 1), pltpu.roll(v, 1, 1))
    return v + jnp.where(lane % 4 < 2, pltpu.roll(v, C - 2, 1), pltpu.roll(v, 2, 1))


def _fold(v):
    return v.reshape(v.shape[0] // SL, SL, C).sum(0)


def _fold_inner(v):
    it = lax.broadcasted_iota(jnp.int32, (SL, C), 0)
    return _fold(v[SL:-SL]) + jnp.where(it == 0, ZERO, v[:SL]) + jnp.where(it == SL - 1, ZERO, v[-SL:])


def _kernel(nh, nw, th, tw, x_hbm, g_hbm, w1v, w2v, gam_ref, bet_ref,
            y_ref, dx_ref, dw1_ref, dw2_ref, dgam_ref, dbet_ref,
            xv, gv, wc1, wt1, wc2, wt2, ucat, gcat, zcat, gt, dat, av, dn, row,
            hr, hc, hk, hrd, hcd, hkd, ec,
            st, sbuf, tt, tbuf, dwl, rd, rxy, zb,
            ld, hs, hv, ss, sr, rs, rr):
    w = lax.axis_index('w')
    h = lax.axis_index('h')
    ndev = nh * nw
    me = w * nh + h
    cnt = float(th * nh * tw * nw * (C // GROUPS))

    barrier = pltpu.get_barrier_semaphore()

    def others():
        for dw in range(nw - 1, -1, -1):
            for dh in range(nh - 1, -1, -1):
                if dw or dh:
                    yield lax.rem(w + dw, nw), h ^ dh

    for dev in others():
        pl.semaphore_signal(barrier, inc=1, device_id=dev, device_id_type=MESH)

    loads = [pltpu.make_async_copy(s, d, ld.at[i]) for i, (s, d) in enumerate(
        ((x_hbm, xv), (g_hbm, gv)))]
    for c in loads:
        c.start()

    def neighbour(d):
        dy, dx = DIRS[d]
        hh, ww = h + dy, w + dx
        ok = (hh >= 0) & (hh < nh) & (ww >= 0) & (ww < nw)
        return ok, (ww, hh)

    def bufs(t):
        return (hr.at[t], hc.at[t], hk.at[t]) if t < 3 else (hrd, hcd, hkd)

    def halo(t, rows, start):
        cols = ec.at[t]
        hrow, hcol, hcor = bufs(t)
        for d, (dy, dx) in enumerate(DIRS):
            ok, dev = neighbour(d)
            o = OPP[d]
            r = 0 if dy < 0 else th - 1
            if dx == 0:
                src, dst = rows.at[r], hrow.at[o]
            elif dy == 0:
                src, dst = cols.at[d - 2], hcol.at[o - 2]
            else:
                src, dst = rows.at[r, pl.ds(0 if dx < 0 else tw - TB, TB)], hcor.at[o - 4]
            cp = pltpu.make_async_remote_copy(src, dst, hs.at[t, d], hv.at[t, o], device_id=dev, device_id_type=MESH)
            if start:
                pl.when(ok)(cp.start)
            else:
                back = pltpu.make_async_remote_copy(
                    src, (hrow.at[d] if dx == 0 else hcol.at[d - 2] if dy == 0 else hcor.at[d - 4]),
                    hs.at[t, d], hv.at[t, d], device_id=dev, device_id_type=MESH)

                @pl.when(ok)
                def _():
                    back.wait_send()
                    back.wait_recv()

    okl = [neighbour(d)[0] for d in range(SL)]

    def first(v):
        return v[0]

    def cat_row(cat, r, shifts=(0, 1, 2)):
        for j in range(0, tw, RB):
            for b in shifts:
                cat[r, pl.ds(j, RB), pl.ds(b * C, C)] = row[pl.ds(SL - 1 + b + j, RB), :].astype(BF)

    def shifted(cat):
        @pl.loop(1, th + 1)
        def _(r):
            for j in range(0, tw, RB):
                row[pl.ds(SL + j, RB), :] = cat[r, pl.ds(j, RB), C:C2].astype(F32)
            cat_row(cat, r, (0, 2))

    def set_ends(left, right):
        row[7:SL, :] = left
        row[tw + SL:tw + NT, :] = right

    def patch(cat, r, left, right):
        it = lax.broadcasted_iota(jnp.int32, (TB, C), 0)
        a = cat[r, 0:TB, 0:C].astype(F32)
        cat[r, 0:TB, 0:C] = jnp.where(it == 0, left, a).astype(BF)
        b = cat[r, tw - TB:tw, C2:C3].astype(F32)
        cat[r, tw - TB:tw, C2:C3] = jnp.where(it == 15, right, b).astype(BF)

    def halo_rows(cat, f, *ts):
        hrow, hcol, hcor = zip(*[bufs(t) for t in ts])
        for e, r in ((0, 0), (1, th + 1)):
            for j in range(0, tw, RB):
                row[pl.ds(SL + j, RB), :] = jnp.where(okl[e], f([b[e, pl.ds(j, RB), :].astype(F32) for b in hrow]), ZERO)
            kl, kr = 2 * e, 2 * e + 1
            cl = f([b[kl].astype(F32) for b in hcor])
            cr = f([b[kr].astype(F32) for b in hcor])
            set_ends(jnp.where(okl[4 + kl], cl[15:TB, :], ZERO), jnp.where(okl[4 + kr], cr[0:1, :], ZERO))
            cat_row(cat, r)

        @pl.loop(0, th // SL)
        def _(k):
            r8 = pl.multiple_of(k * SL, SL)
            lf = jnp.where(okl[2], f([b[0, pl.ds(r8, SL), :].astype(F32) for b in hcol]), ZERO)
            rg = jnp.where(okl[3], f([b[1, pl.ds(r8, SL), :].astype(F32) for b in hcol]), ZERO)
            for i in range(SL):
                patch(cat, r8 + i + 1, lf[i:i + 1, :], rg[i:i + 1, :])

    def build(src, cat, t, vt):
        @pl.loop(0, th)
        def _(r):
            for j in range(0, tw, RB):
                row[pl.ds(SL + j, RB), :] = src[r, pl.ds(j, RB), :].astype(F32)
            ec[t, 0, pl.ds(r, 1), :] = row[SL:NT, :]
            ec[t, 1, pl.ds(r, 1), :] = row[tw + 7:tw + SL, :]
            cat_row(cat, r + 1)
            if vt is not None:
                vt[r + 2] = src[r].T

    def weights(wv, wc, wt):
        for r in range(4):
            for b in range(3):
                for t in range(2):
                    a = r - t
                    sl = (pl.ds((r * 3 + b) * C, C), pl.ds(t * C, C))
                    if 0 <= a < 3:
                        wc[sl] = wv[a * 3 + b]
                        wt[sl] = wv[(2 - a) * 3 + 2 - b].T
                    else:
                        wc[sl] = jnp.zeros((C, C), BF)
                        wt[sl] = jnp.zeros((C, C), BF)

    def dot(blocks, wc):
        lhs = jnp.concatenate([jnp.concatenate(list(b), axis=1) for b in blocks], axis=0)
        return jnp.dot(lhs, wc[...], preferred_element_type=F32)

    def conv(cat, wc, lo, hi, carry, fn):
        for r0 in range(lo, hi, SL):
            n = min(SL, hi - r0)
            o = dot([[cat[r0 + p + r] for r in range(4)] for p in range(0, n, 2)], wc)
            carry = fn(range(r0, r0 + n), o, carry)
        return carry

    def rows_of(o):
        return [o[(i // 2) * tw:(i // 2 + 1) * tw, (i % 2) * C:(i % 2 + 1) * C] for i in range(2 * o.shape[0] // tw)]

    def wgrad_ab(vt, cat, dst):
        for k in (0, 1, th + 2, th + 3):
            vt[k] = jnp.zeros((C, tw), BF)
        lhs = jnp.concatenate([
            jnp.concatenate([vt[i + 2 - a] for a in range(3)], axis=0) for i in range(th + 2)], axis=1)
        rhs = cat[:, :, pl.ds(0, C2)].reshape((th + 2) * tw, C2)
        o = jnp.dot(lhs, rhs, preferred_element_type=F32)
        for b in range(2):
            for a in range(3):
                dst[pl.ds((b * 3 + a) * C, C), :] = o[a * C:(a + 1) * C, b * C:(b + 1) * C].T

    def wgrad_c(vt, cat, dst):
        n = pl.ds(C2, C)
        rows = range(0, th + 2, 2)
        lhs = jnp.concatenate([jnp.concatenate([vt[i + r] for r in range(4)], axis=0) for i in rows], axis=1)
        rhs = jnp.concatenate([jnp.concatenate([cat[i, :, n], cat[i + 1, :, n]], axis=1) for i in rows], axis=0)
        o = jnp.dot(lhs, rhs, preferred_element_type=F32)
        for a in range(3):
            v = [o[(t + 2 - a) * C:(t + 3 - a) * C, t * C:(t + 1) * C] for t in range(2)]
            dst[pl.ds((6 + a) * C, C), :] = (v[0] + v[1]).T

    def spread(src, buf, i):
        buf[me] = src[...]
        for dev in others():
            pltpu.make_async_remote_copy(src, buf.at[me], ss.at[i], sr.at[i], device_id=dev, device_id_type=MESH).start()

    def gather(buf, i):
        part = buf.at[pl.ds(0, ndev - 1)]
        pltpu.make_async_copy(part, part, sr.at[i]).wait()
        pltpu.make_async_copy(part, part, ss.at[i]).wait()
        s = buf[0]
        for k in range(1, ndev):
            s = s + buf[k]
        return s

    core, q_me = h % 2, h // 2
    jobs = ((0, 0, 6 * C), (0, 6 * C, C3), (1, 0, NT * C))
    outs = (dw1_ref, dw2_ref)

    def ar_step(i, n):
        k_arr, base, rows = jobs[i]
        src, out = dwl.at[k_arr], outs[k_arr]
        half, piece = rows // 2, rows // 8
        buf = pl.ds(0, piece)

        def sl(c, q=0, n=piece):
            return pl.ds(pl.multiple_of(base + c * half + q * piece, SL), n)

        def cp(a, b, k, dev):
            return pltpu.make_async_remote_copy(a, b, rs.at[i, k], rr.at[i, k], device_id=dev, device_id_type=MESH)

        peer = (w, h ^ 1)
        xy = [(k, (w, h ^ (2 * k))) for k in range(1, 4)]
        zs = [(k, lax.rem(w + k, nw), lax.rem(w + nw - k, nw)) for k in range(1, nw)]
        mine = sl(core, q_me)
        pair_rs = cp(src.at[sl(1 - core, 0, half)], rd.at[i, pl.ds(0, half)], 0, peer)
        xy_rs = [cp(src.at[sl(core, q_me ^ k)], rxy.at[i, k - 1, buf], k, dev) for k, dev in xy]
        zslot = zb.at[i, w, buf]
        z_out = [cp(zslot, zslot, 3 + k, (to, h)) for k, to, _ in zs]
        z_in = [cp(zslot, zb.at[i, fr, buf], 3 + k, peer) for k, _, fr in zs]
        xy_out = [cp(out.at[mine], out.at[mine], 6 + k, dev) for k, dev in xy]
        xy_in = [cp(out.at[mine], out.at[sl(core, q_me ^ k)], 6 + k, peer) for k, _ in xy]
        own = out.at[sl(core, 0, half)]
        pair_out = cp(own, own, 10, peer)
        pair_in = cp(own, out.at[sl(1 - core, 0, half)], 10, peer)

        def begin(cps):
            for c in cps:
                c.start()

        def end(sent, got):
            for c in sent:
                c.wait_send()
            for c in got:
                c.wait_recv()

        if n == 0:
            begin([pair_rs])
        elif n == 1:
            end([pair_rs], [pair_rs])
            for k in range(4):
                src[sl(core, k), :] = src[sl(core, k), :] + rd[i, pl.ds(k * piece, piece), :]
            begin(xy_rs)
        elif n == 2:
            end(xy_rs, xy_rs)
            zb[i, w, buf] = src[mine, :] + rxy[i, 0, buf] + rxy[i, 1, buf] + rxy[i, 2, buf]
            begin(z_out)
        elif n == 3:
            end(z_out, z_in)
            v = zb[i, 0, buf]
            for k in range(1, nw):
                v = v + zb[i, k, buf]
            out[mine, :] = v
            begin(xy_out)
        elif n == 4:
            end(xy_out, xy_in)
            begin([pair_out])
        else:
            end([pair_out], [pair_in])

    z8 = jnp.zeros((SL, C), F32)
    set_ends(z8[0:1], z8[0:1])
    weights(w1v, wc1, wt1)
    loads[0].wait()
    build(xv, ucat, 0, None)

    def fin_a(rows, o, carry):
        s1, s2 = carry
        for r, v in zip(rows, rows_of(o)):
            vb = v.astype(BF)
            av[r] = vb
            vf = vb.astype(F32)
            s1 = s1 + _fold_inner(vf)
            s2 = s2 + _fold_inner(vf * vf)
        return s1, s2

    sums = conv(ucat, wc1, 2, th // 2 + 2, (z8, z8), fin_a)
    pl.semaphore_wait(barrier, ndev - 1)
    halo(0, xv, True)
    sums = conv(ucat, wc1, th // 2 + 2, th - 2, sums, fin_a)

    weights(w2v, wc2, wt2)
    loads[1].wait()
    build(gv, gcat, 1, gt)
    halo(1, gv, True)

    halo(0, xv, False)
    halo_rows(ucat, first, 0)
    o = dot([[ucat[p + r] for r in range(4)] for p in (0, th - 2)], wc1)
    s1, s2 = fin_a((0, 1, th - 2, th - 1), o, sums)
    it = lax.broadcasted_iota(jnp.int32, (TB, C), 0)
    sides = (pl.ds(0, TB), pl.ds(tw - TB, TB))
    o = dot([[ucat[p + r, s] for r in range(4)] for p in range(0, th, 2) for s in sides], wc1)
    for p in range(th):
        for e, s in enumerate(sides):
            k = (p // 2) * 2 + e
            vb = o[k * TB:(k + 1) * TB, (p % 2) * C:(p % 2 + 1) * C].astype(BF)
            av[p, s] = vb
            vf = jnp.where(it == e * (TB - 1), vb.astype(F32), ZERO)
            ec[2, e, p:p + 1, :] = vf[e * (TB - 1):e * (TB - 1) + 1, :]
            s1 = s1 + _fold(vf)
            s2 = s2 + _fold(vf * vf)
    st[0:1, :] = s1.sum(0, keepdims=True)
    st[1:2, :] = s2.sum(0, keepdims=True)
    spread(st, sbuf, 0)
    halo(2, av, True)

    halo(1, gv, False)
    halo_rows(gcat, first, 1)

    def fin_dz(rows, o, carry):
        for r, v in zip(rows, rows_of(o)):
            dn[r] = v
        return carry

    conv(gcat, wt2, 0, th, 0, fin_dz)

    tot = _group_sum(gather(sbuf, 0)) / cnt
    mean = tot[0:1, :]
    rstd = lax.rsqrt(tot[1:2, :] - mean * mean + EPS)
    sh = -mean * rstd
    gam = gam_ref[...]
    bet = bet_ref[...]

    def act(a):
        xh = a * rstd + sh
        n = xh * gam + bet
        n2 = n * n
        p = 0.5 + 0.5 * jnp.tanh(n * (GC + GC2 * n2))
        return xh, n2, p, n * p

    def zrow(r, carry):
        t0, t1 = carry
        for j in range(0, tw, RB):
            s = pl.ds(j, RB)
            xh, n2, p, z = act(av[r, s, :].astype(F32))
            zcat[r + 1, s, C:C2] = z.astype(BF)
            d = dn[r, s, :] * (p + z * (1.0 - p) * (2.0 * GC + 6.0 * GC2 * n2))
            dn[r, s, :] = d
            if j == 0:
                ec[3, 0, pl.ds(r, 1), :] = d[0:1, :]
            if j + RB == tw:
                ec[3, 1, pl.ds(r, 1), :] = d[RB - 1:RB, :]
            t0 = t0 + _fold(d * xh)
            t1 = t1 + _fold(d)
        return t0, t1

    t0, t1 = lax.fori_loop(0, th, zrow, (z8, z8))
    tt[0:1, :] = t0.sum(0, keepdims=True)
    tt[1:2, :] = t1.sum(0, keepdims=True)
    spread(tt, tbuf, 1)
    halo(3, dn, True)

    shifted(zcat)
    halo(2, av, False)
    halo_rows(zcat, lambda v: act(v[0])[3], 2)
    wgrad_ab(gt, zcat, dwl.at[1])
    wgrad_c(gt, zcat, dwl.at[1])
    ar_step(2, 0)

    t = gather(tbuf, 1)
    dgam_ref[...] = t[0:1, :]
    dbet_ref[...] = t[1:2, :]
    u = _group_sum(t * gam) / cnt
    k1 = gam * rstd
    k2 = -rstd * rstd * u[0:1, :]
    k3 = -rstd * (u[1:2, :] + sh * u[0:1, :])

    @pl.loop(0, th)
    def _(r):
        for j in range(0, tw, RB):
            s = pl.ds(j, RB)
            v = (dn[r, s, :] * k1 + av[r, s, :].astype(F32) * k2 + k3).astype(BF)
            gcat[r + 1, s, C:C2] = v
        dat[r + 2] = gcat[r + 1, :, C:C2].T

    ar_step(2, 1)

    wgrad_ab(dat, ucat, dwl.at[0])
    ar_step(0, 0)
    wgrad_c(dat, ucat, dwl.at[0])
    ar_step(0, 1)
    ar_step(1, 0)
    ar_step(2, 2)

    shifted(gcat)
    halo(3, dn, False)
    halo_rows(gcat, lambda v: v[0] * k1 + v[1] * k2 + k3, 3, 2)
    ar_step(1, 1)

    def fin_dx(rows, o, carry):
        for r, v in zip(rows, rows_of(o)):
            dx_ref[r] = (v + gv[r].astype(F32)).astype(BF)
        return carry

    def fin_y(rows, o, carry):
        for r, v in zip(rows, rows_of(o)):
            y_ref[r] = (v + xv[r].astype(F32)).astype(BF)
        return carry

    conv(gcat, wt1, 0, th, 0, fin_dx)
    ar_step(2, 3)
    ar_step(0, 2)
    conv(zcat, wc2, 0, th // 4, 0, fin_y)
    ar_step(1, 2)
    conv(zcat, wc2, th // 4, th, 0, fin_y)
    ar_step(2, 4)
    for n in range(3, 6):
        ar_step(0, n)
        ar_step(1, n)
        if n == 3:
            ar_step(2, 5)


def _flush(n, *refs):
    ins, res, sem = refs[:n], refs[n:2 * n], refs[-1]
    cps = []
    for i in range(n):
        if res[i].shape == ins[i].shape:
            cps.append((ins[i], res[i]))
        else:
            cps += [(ins[i].at[pl.ds((k % 3 * 3 + k // 3) * C, C)], res[i].at[k]) for k in range(NT)]
    cps = [pltpu.make_async_copy(a, b, sem.at[k]) for k, (a, b) in enumerate(cps)]
    for c in cps:
        c.start()
    for c in cps:
        c.wait()


def solution(mesh):
    nh, nw = mesh.shape['h'], mesh.shape['w']
    tile = P(None, 'h', 'w', None)

    def body(x, w1, gamma, beta, w2, g):
        _, th, tw, c = x.shape
        hbm = pl.BlockSpec(memory_space=pltpu.HBM)
        vm = pl.BlockSpec(memory_space=pltpu.VMEM)
        V = pltpu.VMEM
        D = pltpu.SemaphoreType.DMA
        img = jax.ShapeDtypeStruct((th, tw, c), BF)
        wsh = jax.ShapeDtypeStruct((NT * c, c), F32)
        wsp = jax.ShapeDtypeStruct((NT, c, c), F32)
        vec = jax.ShapeDtypeStruct((1, c), F32)
        cat = V((th + 2, tw, 3 * c), BF)
        ndev = nh * nw
        scratch = dict(
            xv=V((th, tw, c), BF), gv=V((th, tw, c), BF),
            wc1=V((12 * c, 2 * c), BF), wt1=V((12 * c, 2 * c), BF), wc2=V((12 * c, 2 * c), BF), wt2=V((12 * c, 2 * c), BF),
            ucat=cat, gcat=cat, zcat=cat, gt=V((th + 4, c, tw), BF), dat=V((th + 4, c, tw), BF),
            av=V((th, tw, c), BF), dn=V((th, tw, c), F32), row=V((tw + TB, c), F32),
            hr=V((3, 2, tw, c), BF), hc=V((3, 2, th, c), F32), hk=V((3, 4, TB, c), BF),
            hrd=V((2, tw, c), F32), hcd=V((2, th, c), F32), hkd=V((4, TB, c), F32), ec=V((4, 2, th, c), F32),
            st=V((2, c), F32), sbuf=V((ndev, 2, c), F32), tt=V((2, c), F32), tbuf=V((ndev, 2, c), F32),
            dwl=V((2, NT * c, c), F32),
            rd=V((3, NT * c // 2, c), F32), rxy=V((3, 3, NT * c // SL, c), F32), zb=V((3, nw, NT * c // SL, c), F32),
            ld=D((2,)), hs=D((4, SL)), hv=D((4, SL)), ss=D((2,)), sr=D((2,)), rs=D((3, 11)), rr=D((3, 11)),
        )
        res = pl.pallas_call(
            functools.partial(_kernel, nh, nw, th, tw),
            out_shape=(img, img, wsh, wsh, vec, vec),
            in_specs=[hbm] * 2 + [vm] * 4,
            out_specs=(vm,) * 6,
            scratch_shapes=list(scratch.values()),
            compiler_params=pltpu.CompilerParams(collective_id=0, has_side_effects=True, vmem_limit_bytes=48 << 20),
        )(x.reshape(th, tw, c), g.reshape(th, tw, c), w1.reshape(NT, c, c), w2.reshape(NT, c, c),
          gamma.reshape(1, c), beta.reshape(1, c))
        y, dx, dw1, dw2, dg, db = pl.pallas_call(
            functools.partial(_flush, len(res)),
            out_shape=(img, img, wsp, wsp, vec, vec),
            in_specs=[vm] * len(res),
            out_specs=(hbm,) * len(res),
            scratch_shapes=[D((4 + 2 * NT,))],
            compiler_params=pltpu.CompilerParams(vmem_limit_bytes=1 << 20),
        )(*res)
        return (y.reshape(x.shape), dx.reshape(x.shape), dw1.reshape(3, 3, c, c), dw2.reshape(3, 3, c, c),
                dg.reshape(c), db.reshape(c))

    return jax.shard_map(body, mesh=mesh, in_specs=(tile, P(), P(), P(), P(), tile),
                         out_specs=(tile, tile, P(), P(), P(), P()), check_vma=False)
```

time: 70.2 us -> 66.6 us (0.949)
  Pallas kernels: 65.9 us -> 62.4 us
    pallas_call x1, Pallas kernels: 63.5 us -> 59.9 us  [body(): pl.pallas_call(functools.partial(_kernel, nh, nw, th, tw), out_shape=(img...]
where the time goes in v3:
time: 66.6 us; the launch traced here: 66.4 us
  Pallas kernels  62.4 us (94%)
  local copies, waits for them, and re-layouts  3.23 us (5%)
  between operations  0.81 us (1%)
    pallas_call x1, Pallas kernels, body(): pl.pallas_call(functools.partial(_kernel, nh, nw, th, tw), out_shape=(img...  59.9 us
    unnamed x8, local copies, waits for them, and re-layouts  3.23 us
    pallas_call x1, Pallas kernels, body(): pl.pallas_call(functools.partial(_flush, len(res)), out_shape=(img, img,...  2.54 us

profile of v3, /device:TPU:0, one launch (start us, length us, event | category | flops | bytes accessed | tf_op | source)
XLA Modules:
  0.0 66.4 jit_solution(3724539190405656218)
XLA Ops:
  0.6 0.0 copy-start
  0.6 1.0 %copy-done = bf16[3,3,128,128]{3,2,1,0:T(8,128)(2,1)S(1)} copy-done((bf16[3,3,128,128]{3,2,1,0:T(8,128)(2,1)S(1)}, bf16[3,3,128,128]{3,2,1,0:T(8,128)(2,1)}, u32[]{:S(2)}) %copy-start) | copy-done | bytes 294936
  1.6 0.0 copy-start.1
  1.6 1.0 %copy-done.1 = bf16[3,3,128,128]{3,2,1,0:T(8,128)(2,1)S(1)} copy-done((bf16[3,3,128,128]{3,2,1,0:T(8,128)(2,1)S(1)}, bf16[3,3,128,128]{3,2,1,0:T(8,128)(2,1)}, u32[]{:S(2)}) %copy-start.1) | copy-done | bytes 294936
  2.6 0.0 copy-start.2
  2.6 0.7 copy-done.2
  3.2 0.0 copy-start.3
  3.2 0.7 copy-done.3
  3.9 59.9 %shard_map.109 = (bf16[32,256,128]{2,1,0:T(8,128)(2,1)S(1)}, bf16[32,256,128]{2,1,0:T(8,128)(2,1)S(1)}, f32[1152,128]{1,0:T(8,128)S(1)}, f32[1152,128]{1,0:T(8,1...) custom-call(bf16[32,256,128]{2,1,0:T(8,128)(2,1)} %bitcast.16, bf16[32,256,128]{2,1,0:T(8,128)(2,1)} %bitcast.17, ...), custom_call_target="tpu_custom_call" | custom-call | tf_op jit(solution)/shard_map/pallas_call | solution.py:484
  63.7 2.5 %shard_map.110 = (bf16[32,256,128]{2,1,0:T(8,128)(2,1)}, bf16[32,256,128]{2,1,0:T(8,128)(2,1)}, f32[9,128,128]{2,1,0:T(8,128)}, f32[9,128,128]{2,1,0:T(8,128)}, f32[1,128]{1,0:T(1,128)}, /*index=5*/f32[1,128]{1,0:T(1,128)}) custom-call(bf16[32,256,128]{2,1,0:T(8,128)(2,1)S(1)} %get-tuple-element.18.refs_0_, ...), custom_call_target="tpu_custom_call" | custom-call | tf_op jit(solution)/shard_map/pallas_call | solution.py:493
Async XLA Ops:
  0.6 1.0 %copy-start = (bf16[3,3,128,128]{3,2,1,0:T(8,128)(2,1)S(1)}, bf16[3,3,128,128]{3,2,1,0:T(8,128)(2,1)}, u32[]{:S(2)}) copy-start(bf16[3,3,128,128]{3,2,1,0:T(8,128)(2,1)} %param.7) | copy-start | bytes 884740
  1.6 1.0 %copy-start.1 = (bf16[3,3,128,128]{3,2,1,0:T(8,128)(2,1)S(1)}, bf16[3,3,128,128]{3,2,1,0:T(8,128)(2,1)}, u32[]{:S(2)}) copy-start(bf16[3,3,128,128]{3,2,1,0:T(8,128)(2,1)} %param.10) | copy-start | bytes 884740
  2.6 0.7 copy-start.2
  3.2 0.7 copy-start.3

commit v4 on v3

--- a/solution.py
+++ b/solution.py
@@ -40,7 +40,7 @@
             y_ref, dx_ref, dw1_ref, dw2_ref, dgam_ref, dbet_ref,
             xv, gv, wc1, wt1, wc2, wt2, ucat, gcat, zcat, gt, dat, av, dn, row,
             hr, hc, hk, hrd, hcd, hkd, ec,
-            st, sbuf, tt, tbuf, dwl, rd, rxy, zb,
+            st, sbuf, tt, tbuf, dwl, rd, rxy, zx_buf,
             ld, hs, hv, ss, sr, rs, rr):
     w = lax.axis_index('w')
     h = lax.axis_index('h')
@@ -79,7 +79,7 @@
         for d, (dy, dx) in enumerate(DIRS):
             ok, dev = neighbour(d)
             o = OPP[d]
-            r = 0 if dy < 0 else th - 1
+            r = 0 if dy < 0 else rows.shape[0] - 1
             if dx == 0:
                 src, dst = rows.at[r], hrow.at[o]
             elif dy == 0:
@@ -146,29 +146,23 @@
             for i in range(SL):
                 patch(cat, r8 + i + 1, lf[i:i + 1, :], rg[i:i + 1, :])
 
-    def build(src, cat, t, vt):
+    def build(src, cat, t):
         @pl.loop(0, th)
         def _(r):
             for j in range(0, tw, RB):
                 row[pl.ds(SL + j, RB), :] = src[r, pl.ds(j, RB), :].astype(F32)
             ec[t, 0, pl.ds(r, 1), :] = row[SL:NT, :]
-            ec[t, 1, pl.ds(r, 1), :] = row[tw + 7:tw + SL, :]
+            ec[t, 1, pl.ds(r, 1), :] = row[tw + SL - 1:tw + SL, :]
             cat_row(cat, r + 1)
-            if vt is not None:
-                vt[r + 2] = src[r].T
-
-    def weights(wv, wc, wt):
+
+    def weights(wv, wc, flip):
         for r in range(4):
             for b in range(3):
                 for t in range(2):
-                    a = r - t
-                    sl = (pl.ds((r * 3 + b) * C, C), pl.ds(t * C, C))
-                    if 0 <= a < 3:
-                        wc[sl] = wv[a * 3 + b]
-                        wt[sl] = wv[(2 - a) * 3 + 2 - b].T
-                    else:
-                        wc[sl] = jnp.zeros((C, C), BF)
-                        wt[sl] = jnp.zeros((C, C), BF)
+                    k = (r - t) * 3 + b
+                    ok = t <= r < t + 3
+                    v = jnp.zeros((C, C), BF) if not ok else wv[NT - 1 - k].T if flip else wv[k]
+                    wc[pl.ds((r * 3 + b) * C, C), pl.ds(t * C, C)] = v
 
     def dot(blocks, wc):
         lhs = jnp.concatenate([jnp.concatenate(list(b), axis=1) for b in blocks], axis=0)
@@ -237,13 +231,13 @@
 
         peer = (w, h ^ 1)
         xy = [(k, (w, h ^ (2 * k))) for k in range(1, 4)]
-        zs = [(k, lax.rem(w + k, nw), lax.rem(w + nw - k, nw)) for k in range(1, nw)]
+        zp = [(k, lax.rem(w + k, nw), lax.rem(w + nw - k, nw)) for k in range(1, nw)]
         mine = sl(core, q_me)
         pair_rs = cp(src.at[sl(1 - core, 0, half)], rd.at[i, pl.ds(0, half)], 0, peer)
         xy_rs = [cp(src.at[sl(core, q_me ^ k)], rxy.at[i, k - 1, buf], k, dev) for k, dev in xy]
-        zslot = zb.at[i, w, buf]
-        z_out = [cp(zslot, zslot, 3 + k, (to, h)) for k, to, _ in zs]
-        z_in = [cp(zslot, zb.at[i, fr, buf], 3 + k, peer) for k, _, fr in zs]
+        zx = zx_buf.at[i]
+        zx_out = [cp(zx.at[w, buf], zx.at[w, buf], 3 + k, (to, h)) for k, to, _ in zp]
+        zx_in = [cp(zx.at[w, buf], zx.at[fr, buf], 3 + k, peer) for k, _, fr in zp]
         xy_out = [cp(out.at[mine], out.at[mine], 6 + k, dev) for k, dev in xy]
         xy_in = [cp(out.at[mine], out.at[sl(core, q_me ^ k)], 6 + k, peer) for k, _ in xy]
         own = out.at[sl(core, 0, half)]
@@ -269,13 +263,13 @@
             begin(xy_rs)
         elif n == 2:
             end(xy_rs, xy_rs)
-            zb[i, w, buf] = src[mine, :] + rxy[i, 0, buf] + rxy[i, 1, buf] + rxy[i, 2, buf]
-            begin(z_out)
+            zx[w, buf] = src[mine, :] + rxy[i, 0, buf] + rxy[i, 1, buf] + rxy[i, 2, buf]
+            begin(zx_out)
         elif n == 3:
-            end(z_out, z_in)
-            v = zb[i, 0, buf]
+            end(zx_out, zx_in)
+            v = zx[0, buf]
             for k in range(1, nw):
-                v = v + zb[i, k, buf]
+                v = v + zx[k, buf]
             out[mine, :] = v
             begin(xy_out)
         elif n == 4:
@@ -286,9 +280,9 @@
 
     z8 = jnp.zeros((SL, C), F32)
     set_ends(z8[0:1], z8[0:1])
-    weights(w1v, wc1, wt1)
+    weights(w1v, wc1, False)
     loads[0].wait()
-    build(xv, ucat, 0, None)
+    build(xv, ucat, 0)
 
     def fin_a(rows, o, carry):
         s1, s2 = carry
@@ -305,9 +299,9 @@
     halo(0, xv, True)
     sums = conv(ucat, wc1, th // 2 + 2, th - 2, sums, fin_a)
 
-    weights(w2v, wc2, wt2)
+    weights(w2v, wt2, True)
     loads[1].wait()
-    build(gv, gcat, 1, gt)
+    build(gv, gcat, 1)
     halo(1, gv, True)
 
     halo(0, xv, False)
@@ -331,6 +325,10 @@
     spread(st, sbuf, 0)
     halo(2, av, True)
 
+    @pl.loop(0, th)
+    def _(r):
+        gt[r + 2] = gv[r].T
+
     halo(1, gv, False)
     halo_rows(gcat, first, 1)
 
@@ -392,21 +390,25 @@
     k2 = -rstd * rstd * u[0:1, :]
     k3 = -rstd * (u[1:2, :] + sh * u[0:1, :])
 
-    @pl.loop(0, th)
-    def _(r):
-        for j in range(0, tw, RB):
-            s = pl.ds(j, RB)
-            v = (dn[r, s, :] * k1 + av[r, s, :].astype(F32) * k2 + k3).astype(BF)
-            gcat[r + 1, s, C:C2] = v
-        dat[r + 2] = gcat[r + 1, :, C:C2].T
-
+    def da_rows(lo, hi):
+        @pl.loop(lo, hi)
+        def _(r):
+            for j in range(0, tw, RB):
+                s = pl.ds(j, RB)
+                v = (dn[r, s, :] * k1 + av[r, s, :].astype(F32) * k2 + k3).astype(BF)
+                gcat[r + 1, s, C:C2] = v
+            dat[r + 2] = gcat[r + 1, :, C:C2].T
+
+    da_rows(0, 3 * th // 4)
     ar_step(2, 1)
+    da_rows(3 * th // 4, th)
 
     wgrad_ab(dat, ucat, dwl.at[0])
     ar_step(0, 0)
     wgrad_c(dat, ucat, dwl.at[0])
     ar_step(0, 1)
     ar_step(1, 0)
+    weights(w1v, wt1, True)
     ar_step(2, 2)
 
     shifted(gcat)
@@ -424,18 +426,16 @@
             y_ref[r] = (v + xv[r].astype(F32)).astype(BF)
         return carry
 
+    t8 = th // 4
     conv(gcat, wt1, 0, th, 0, fin_dx)
+    weights(w2v, wc2, False)
     ar_step(2, 3)
     ar_step(0, 2)
-    conv(zcat, wc2, 0, th // 4, 0, fin_y)
+    conv(zcat, wc2, 0, t8, 0, fin_y)
     ar_step(1, 2)
-    conv(zcat, wc2, th // 4, th, 0, fin_y)
-    ar_step(2, 4)
-    for n in range(3, 6):
-        ar_step(0, n)
-        ar_step(1, n)
-        if n == 3:
-            ar_step(2, 5)
+    conv(zcat, wc2, t8, th, 0, fin_y)
+    for i, n in ((2, 4), (0, 3), (1, 3), (2, 5), (0, 4), (1, 4), (0, 5), (1, 5)):
+        ar_step(i, n)
 
 
 def _flush(n, *refs):
@@ -478,7 +478,7 @@
             hrd=V((2, tw, c), F32), hcd=V((2, th, c), F32), hkd=V((4, TB, c), F32), ec=V((4, 2, th, c), F32),
             st=V((2, c), F32), sbuf=V((ndev, 2, c), F32), tt=V((2, c), F32), tbuf=V((ndev, 2, c), F32),
             dwl=V((2, NT * c, c), F32),
-            rd=V((3, NT * c // 2, c), F32), rxy=V((3, 3, NT * c // SL, c), F32), zb=V((3, nw, NT * c // SL, c), F32),
+            rd=V((3, NT * c // 2, c), F32), rxy=V((3, 3, NT * c // SL, c), F32), zx_buf=V((3, nw, NT * c // SL, c), F32),
             ld=D((2,)), hs=D((4, SL)), hv=D((4, SL)), ss=D((2,)), sr=D((2,)), rs=D((3, 11)), rr=D((3, 11)),
         )
         res = pl.pallas_call(

time: 66.6 us -> 65.2 us (0.979)
  Pallas kernels: 62.4 us -> 61 us
    pallas_call x1, Pallas kernels: 59.9 us -> 58.5 us  [body(): pl.pallas_call(functools.partial(_kernel, nh, nw, th, tw), out_shape=(img...]
where the time goes in v4:
time: 65.2 us; the launch traced here: 65 us
  Pallas kernels  61 us (94%)
  local copies, waits for them, and re-layouts  3.23 us (5%)
  between operations  0.81 us (1%)
    pallas_call x1, Pallas kernels, body(): pl.pallas_call(functools.partial(_kernel, nh, nw, th, tw), out_shape=(img...  58.5 us
    unnamed x8, local copies, waits for them, and re-layouts  3.23 us
    pallas_call x1, Pallas kernels, body(): pl.pallas_call(functools.partial(_flush, len(res)), out_shape=(img, img,...  2.54 us

profile of v4, /device:TPU:0, one launch (start us, length us, event | category | flops | bytes accessed | tf_op | source)
XLA Modules:
  0.0 65.0 jit_solution(8057634371467531972)
XLA Ops:
  0.6 0.0 copy-start
  0.6 1.0 %copy-done = bf16[3,3,128,128]{3,2,1,0:T(8,128)(2,1)S(1)} copy-done((bf16[3,3,128,128]{3,2,1,0:T(8,128)(2,1)S(1)}, bf16[3,3,128,128]{3,2,1,0:T(8,128)(2,1)}, u32[]{:S(2)}) %copy-start) | copy-done | bytes 294936
  1.6 0.0 copy-start.1
  1.6 1.0 %copy-done.1 = bf16[3,3,128,128]{3,2,1,0:T(8,128)(2,1)S(1)} copy-done((bf16[3,3,128,128]{3,2,1,0:T(8,128)(2,1)S(1)}, bf16[3,3,128,128]{3,2,1,0:T(8,128)(2,1)}, u32[]{:S(2)}) %copy-start.1) | copy-done | bytes 294936
  2.6 0.0 copy-start.2
  2.6 0.7 %copy-done.2 = f32[128]{0:T(128)S(1)} copy-done((f32[128]{0:T(128)S(1)}, f32[128]{0:T(128)}, u32[]{:S(2)}) %copy-start.2) | copy-done | bytes 536
  3.2 0.0 copy-start.3
  3.2 0.7 %copy-done.3 = f32[128]{0:T(128)S(1)} copy-done((f32[128]{0:T(128)S(1)}, f32[128]{0:T(128)}, u32[]{:S(2)}) %copy-start.3) | copy-done | bytes 536
  3.9 58.5 %shard_map.109 = (bf16[32,256,128]{2,1,0:T(8,128)(2,1)S(1)}, bf16[32,256,128]{2,1,0:T(8,128)(2,1)S(1)}, f32[1152,128]{1,0:T(8,128)S(1)}, f32[1152,128]{1,0:T(8,1...) custom-call(bf16[32,256,128]{2,1,0:T(8,128)(2,1)} %bitcast.16, bf16[32,256,128]{2,1,0:T(8,128)(2,1)} %bitcast.17, ...), custom_call_target="tpu_custom_call" | custom-call | tf_op jit(solution)/shard_map/pallas_call | solution.py:484
  62.3 2.5 %shard_map.110 = (bf16[32,256,128]{2,1,0:T(8,128)(2,1)}, bf16[32,256,128]{2,1,0:T(8,128)(2,1)}, f32[9,128,128]{2,1,0:T(8,128)}, f32[9,128,128]{2,1,0:T(8,128)}, f32[1,128]{1,0:T(1,128)}, /*index=5*/f32[1,128]{1,0:T(1,128)}) custom-call(bf16[32,256,128]{2,1,0:T(8,128)(2,1)S(1)} %get-tuple-element.18.refs_0_, ...), custom_call_target="tpu_custom_call" | custom-call | tf_op jit(solution)/shard_map/pallas_call | solution.py:493
Async XLA Ops:
  0.6 1.0 %copy-start = (bf16[3,3,128,128]{3,2,1,0:T(8,128)(2,1)S(1)}, bf16[3,3,128,128]{3,2,1,0:T(8,128)(2,1)}, u32[]{:S(2)}) copy-start(bf16[3,3,128,128]{3,2,1,0:T(8,128)(2,1)} %param.7) | copy-start | bytes 884740
  1.6 1.0 %copy-start.1 = (bf16[3,3,128,128]{3,2,1,0:T(8,128)(2,1)S(1)}, bf16[3,3,128,128]{3,2,1,0:T(8,128)(2,1)}, u32[]{:S(2)}) copy-start(bf16[3,3,128,128]{3,2,1,0:T(8,128)(2,1)} %param.10) | copy-start | bytes 884740
  2.6 0.7 %copy-start.2 = (f32[128]{0:T(128)S(1)}, f32[128]{0:T(128)}, u32[]{:S(2)}) copy-start(f32[128]{0:T(128)} %param.8) | copy-start | bytes 1540
  3.2 0.7 %copy-start.3 = (f32[128]{0:T(128)S(1)}, f32[128]{0:T(128)}, u32[]{:S(2)}) copy-start(f32[128]{0:T(128)} %param.9) | copy-start | bytes 1540

commit v5 on v4

--- a/solution.py
+++ b/solution.py
@@ -36,7 +36,7 @@
     return _fold(v[SL:-SL]) + jnp.where(it == 0, ZERO, v[:SL]) + jnp.where(it == SL - 1, ZERO, v[-SL:])
 
 
-def _kernel(nh, nw, th, tw, x_hbm, g_hbm, w1v, w2v, gam_ref, bet_ref,
+def _kernel(nh, nw, th, tw, x_hbm, g_hbm, w12, gb,
             y_ref, dx_ref, dw1_ref, dw2_ref, dgam_ref, dbet_ref,
             xv, gv, wc1, wt1, wc2, wt2, ucat, gcat, zcat, gt, dat, av, dn, row,
             hr, hc, hk, hrd, hcd, hkd, ec,
@@ -46,6 +46,7 @@
     h = lax.axis_index('h')
     ndev = nh * nw
     me = w * nh + h
+    w1v, w2v = w12.at[pl.ds(0, NT)], w12.at[pl.ds(NT, NT)]
     cnt = float(th * nh * tw * nw * (C // GROUPS))
 
     barrier = pltpu.get_barrier_semaphore()
@@ -343,8 +344,7 @@
     mean = tot[0:1, :]
     rstd = lax.rsqrt(tot[1:2, :] - mean * mean + EPS)
     sh = -mean * rstd
-    gam = gam_ref[...]
-    bet = bet_ref[...]
+    gam, bet = gb[0:1, :], gb[1:2, :]
 
     def act(a):
         xh = a * rstd + sh
@@ -484,12 +484,12 @@
         res = pl.pallas_call(
             functools.partial(_kernel, nh, nw, th, tw),
             out_shape=(img, img, wsh, wsh, vec, vec),
-            in_specs=[hbm] * 2 + [vm] * 4,
+            in_specs=[hbm] * 2 + [vm] * 2,
             out_specs=(vm,) * 6,
             scratch_shapes=list(scratch.values()),
             compiler_params=pltpu.CompilerParams(collective_id=0, has_side_effects=True, vmem_limit_bytes=48 << 20),
-        )(x.reshape(th, tw, c), g.reshape(th, tw, c), w1.reshape(NT, c, c), w2.reshape(NT, c, c),
-          gamma.reshape(1, c), beta.reshape(1, c))
+        )(x.reshape(th, tw, c), g.reshape(th, tw, c), jnp.concatenate([w1, w2]).reshape(2 * NT, c, c),
+          jnp.stack([gamma, beta]))
         y, dx, dw1, dw2, dg, db = pl.pallas_call(
             functools.partial(_flush, len(res)),
             out_shape=(img, img, wsp, wsp, vec, vec),

time: 65.2 us -> 63.6 us (0.975)
  local copies, waits for them, and re-layouts: 3.23 us -> 0 us
  other arithmetic: 0 us -> 1.78 us
    unnamed x8 -> x0, local copies, waits for them, and re-layouts: 3.23 us -> none
    concatenate x0 -> x1, other arithmetic: none -> 1.1 us  [body(): jnp.concatenate([w1, w2]).reshape(2 * NT, c, c)]
    another operation x0 -> x1, other arithmetic: none -> 0.68 us  [body(): jnp.stack([gamma, beta])]
where the time goes in v5:
time: 63.6 us; the launch traced here: 63.4 us
  Pallas kernels  60.8 us (96%)
  other arithmetic  1.78 us (3%)
  between operations  0.8 us (1%)
    pallas_call x1, Pallas kernels, body(): pl.pallas_call(functools.partial(_kernel, nh, nw, th, tw), out_shape=(img...  58.3 us
    pallas_call x1, Pallas kernels, body(): pl.pallas_call(functools.partial(_flush, len(res)), out_shape=(img, img,...  2.54 us

profile of v5, /device:TPU:0, one launch (start us, length us, event | category | flops | bytes accessed | tf_op | source)
XLA Modules:
  0.0 63.4 jit_solution(6456954266798268260)
XLA Ops:
  0.6 0.7 %pad_maximum_fusion.1.gb = f32[2,128]{1,0:T(2,128)S(1)} fusion(f32[1,128]{1,0:T(1,128)} %bitcast.14, f32[1,128]{1,0:T(1,128)} %bitcast.15), kind=kLoop, calls=%fused_computation.1 | loop fusion | flops 256 | bytes 2048 | tf_op jit(solution)/shard_map/stack | solution.py:492
  1.3 1.1 %pad_maximum_fusion = bf16[6,3,128,128]{3,2,1,0:T(8,128)(2,1)S(1)} fusion(bf16[3,3,128,128]{3,2,1,0:T(8,128)(2,1)} %param.10, bf16[3,3,128,128]{3,2,1,0:T(8,128)(2,1)} %param.7), kind=kLoop, calls=%fused_computation | loop fusion | flops 294912 | bytes 1179648 | tf_op jit(solution)/shard_map/concatenate | solution.py:491
  2.4 58.3 %shard_map.109 = (bf16[32,256,128]{2,1,0:T(8,128)(2,1)S(1)}, bf16[32,256,128]{2,1,0:T(8,128)(2,1)S(1)}, f32[1152,128]{1,0:T(8,128)S(1)}, f32[1152,128]{1,0:T(8,1...) custom-call(bf16[32,256,128]{2,1,0:T(8,128)(2,1)} %bitcast.12, bf16[32,256,128]{2,1,0:T(8,128)(2,1)} %bitcast.13, ...), custom_call_target="tpu_custom_call" | custom-call | tf_op jit(solution)/shard_map/pallas_call | solution.py:484
  60.7 2.5 %shard_map.110 = (bf16[32,256,128]{2,1,0:T(8,128)(2,1)}, bf16[32,256,128]{2,1,0:T(8,128)(2,1)}, f32[9,128,128]{2,1,0:T(8,128)}, f32[9,128,128]{2,1,0:T(8,128)}, f32[1,128]{1,0:T(1,128)}, /*index=5*/f32[1,128]{1,0:T(1,128)}) custom-call(bf16[32,256,128]{2,1,0:T(8,128)(2,1)S(1)} %get-tuple-element.18.refs_0_, ...), custom_call_target="tpu_custom_call" | custom-call | tf_op jit(solution)/shard_map/pallas_call | solution.py:493

commit v6 on v5

--- a/solution.py
+++ b/solution.py
@@ -215,7 +215,7 @@
         return s
 
     core, q_me = h % 2, h // 2
-    jobs = ((0, 0, 6 * C), (0, 6 * C, C3), (1, 0, NT * C))
+    jobs = ((0, 0, NT * C), (1, 0, NT * C))
     outs = (dw1_ref, dw2_ref)
 
     def ar_step(i, n):
@@ -380,7 +380,7 @@
     halo_rows(zcat, lambda v: act(v[0])[3], 2)
     wgrad_ab(gt, zcat, dwl.at[1])
     wgrad_c(gt, zcat, dwl.at[1])
-    ar_step(2, 0)
+    ar_step(1, 0)
 
     t = gather(tbuf, 1)
     dgam_ref[...] = t[0:1, :]
@@ -400,21 +400,19 @@
             dat[r + 2] = gcat[r + 1, :, C:C2].T
 
     da_rows(0, 3 * th // 4)
-    ar_step(2, 1)
+    ar_step(1, 1)
     da_rows(3 * th // 4, th)
 
     wgrad_ab(dat, ucat, dwl.at[0])
+    wgrad_c(dat, ucat, dwl.at[0])
     ar_step(0, 0)
-    wgrad_c(dat, ucat, dwl.at[0])
+    weights(w1v, wt1, True)
     ar_step(0, 1)
-    ar_step(1, 0)
-    weights(w1v, wt1, True)
-    ar_step(2, 2)
+    ar_step(1, 2)
 
     shifted(gcat)
     halo(3, dn, False)
     halo_rows(gcat, lambda v: v[0] * k1 + v[1] * k2 + k3, 3, 2)
-    ar_step(1, 1)
 
     def fin_dx(rows, o, carry):
         for r, v in zip(rows, rows_of(o)):
@@ -426,15 +424,12 @@
             y_ref[r] = (v + xv[r].astype(F32)).astype(BF)
         return carry
 
-    t8 = th // 4
     conv(gcat, wt1, 0, th, 0, fin_dx)
     weights(w2v, wc2, False)
-    ar_step(2, 3)
+    ar_step(1, 3)
     ar_step(0, 2)
-    conv(zcat, wc2, 0, t8, 0, fin_y)
-    ar_step(1, 2)
-    conv(zcat, wc2, t8, th, 0, fin_y)
-    for i, n in ((2, 4), (0, 3), (1, 3), (2, 5), (0, 4), (1, 4), (0, 5), (1, 5)):
+    conv(zcat, wc2, 0, th, 0, fin_y)
+    for i, n in ((1, 4), (0, 3), (1, 5), (0, 4), (0, 5)):
         ar_step(i, n)
 
 
@@ -478,8 +473,8 @@
             hrd=V((2, tw, c), F32), hcd=V((2, th, c), F32), hkd=V((4, TB, c), F32), ec=V((4, 2, th, c), F32),
             st=V((2, c), F32), sbuf=V((ndev, 2, c), F32), tt=V((2, c), F32), tbuf=V((ndev, 2, c), F32),
             dwl=V((2, NT * c, c), F32),
-            rd=V((3, NT * c // 2, c), F32), rxy=V((3, 3, NT * c // SL, c), F32), zx_buf=V((3, nw, NT * c // SL, c), F32),
-            ld=D((2,)), hs=D((4, SL)), hv=D((4, SL)), ss=D((2,)), sr=D((2,)), rs=D((3, 11)), rr=D((3, 11)),
+            rd=V((2, NT * c // 2, c), F32), rxy=V((2, 3, NT * c // SL, c), F32), zx_buf=V((2, nw, NT * c // SL, c), F32),
+            ld=D((2,)), hs=D((4, SL)), hv=D((4, SL)), ss=D((2,)), sr=D((2,)), rs=D((2, 11)), rr=D((2, 11)),
         )
         res = pl.pallas_call(
             functools.partial(_kernel, nh, nw, th, tw),

time: 63.6 us -> 62.8 us (0.987); the launches traced: 63.4 us -> 61.9 us
  Pallas kernels: 60.8 us -> 59.3 us
    pallas_call x1, Pallas kernels: 58.3 us -> 56.8 us  [body(): pl.pallas_call(functools.partial(_kernel, nh, nw, th, tw), out_shape=(img...]
where the time goes in v6:
time: 62.8 us; the launch traced here: 61.9 us
  Pallas kernels  59.3 us (94%)
  other arithmetic  1.78 us (3%)
  between operations  0.8 us (1%)
    pallas_call x1, Pallas kernels, body(): pl.pallas_call(functools.partial(_kernel, nh, nw, th, tw), out_shape=(img...  56.8 us
    pallas_call x1, Pallas kernels, body(): pl.pallas_call(functools.partial(_flush, len(res)), out_shape=(img, img,...  2.54 us

profile of v6, /device:TPU:0, one launch (start us, length us, event | category | flops | bytes accessed | tf_op | source)
XLA Modules:
  0.0 61.9 jit_solution(2450354533214294161)
XLA Ops:
  0.6 0.7 %pad_maximum_fusion.1.gb = f32[2,128]{1,0:T(2,128)S(1)} fusion(f32[1,128]{1,0:T(1,128)} %bitcast.14, f32[1,128]{1,0:T(1,128)} %bitcast.15), kind=kLoop, calls=%fused_computation.1 | loop fusion | flops 256 | bytes 2048 | tf_op jit(solution)/shard_map/stack | solution.py:487
  1.3 1.1 %pad_maximum_fusion = bf16[6,3,128,128]{3,2,1,0:T(8,128)(2,1)S(1)} fusion(bf16[3,3,128,128]{3,2,1,0:T(8,128)(2,1)} %param.10, bf16[3,3,128,128]{3,2,1,0:T(8,128)(2,1)} %param.7), kind=kLoop, calls=%fused_computation | loop fusion | flops 294912 | bytes 1179648 | tf_op jit(solution)/shard_map/concatenate | solution.py:486
  2.4 56.8 %shard_map.109 = (bf16[32,256,128]{2,1,0:T(8,128)(2,1)S(1)}, bf16[32,256,128]{2,1,0:T(8,128)(2,1)S(1)}, f32[1152,128]{1,0:T(8,128)S(1)}, f32[1152,128]{1,0:T(8,1...) custom-call(bf16[32,256,128]{2,1,0:T(8,128)(2,1)} %bitcast.12, bf16[32,256,128]{2,1,0:T(8,128)(2,1)} %bitcast.13, ...), custom_call_target="tpu_custom_call" | custom-call | tf_op jit(solution)/shard_map/pallas_call | solution.py:479
  59.2 2.5 %shard_map.110 = (bf16[32,256,128]{2,1,0:T(8,128)(2,1)}, bf16[32,256,128]{2,1,0:T(8,128)(2,1)}, f32[9,128,128]{2,1,0:T(8,128)}, f32[9,128,128]{2,1,0:T(8,128)}, f32[1,128]{1,0:T(1,128)}, /*index=5*/f32[1,128]{1,0:T(1,128)}) custom-call(bf16[32,256,128]{2,1,0:T(8,128)(2,1)S(1)} %get-tuple-element.18.refs_0_, ...), custom_call_target="tpu_custom_call" | custom-call | tf_op jit(solution)/shard_map/pallas_call | solution.py:488

commit v7 on v6

--- a/solution.py
+++ b/solution.py
@@ -426,8 +426,8 @@
 
     conv(gcat, wt1, 0, th, 0, fin_dx)
     weights(w2v, wc2, False)
+    ar_step(0, 2)
     ar_step(1, 3)
-    ar_step(0, 2)
     conv(zcat, wc2, 0, th, 0, fin_y)
     for i, n in ((1, 4), (0, 3), (1, 5), (0, 4), (0, 5)):
         ar_step(i, n)

time: 62.8 us -> 62.6 us (level)
  no operation moved by 1% of the time
where the time goes in v7:
time: 62.6 us; the launch traced here: 62.1 us
  Pallas kernels  59.5 us (95%)
  other arithmetic  1.78 us (3%)
  between operations  0.8 us (1%)
    pallas_call x1, Pallas kernels, body(): pl.pallas_call(functools.partial(_kernel, nh, nw, th, tw), out_shape=(img...  57 us
    pallas_call x1, Pallas kernels, body(): pl.pallas_call(functools.partial(_flush, len(res)), out_shape=(img, img,...  2.54 us

profile of v7, /device:TPU:0, one launch (start us, length us, event | category | flops | bytes accessed | tf_op | source)
XLA Modules:
  0.0 62.1 jit_solution(14159423256740417985)
XLA Ops:
  0.6 0.7 %pad_maximum_fusion.1.gb = f32[2,128]{1,0:T(2,128)S(1)} fusion(f32[1,128]{1,0:T(1,128)} %bitcast.14, f32[1,128]{1,0:T(1,128)} %bitcast.15), kind=kLoop, calls=%fused_computation.1 | loop fusion | flops 256 | bytes 2048 | tf_op jit(solution)/shard_map/stack | solution.py:487
  1.3 1.1 %pad_maximum_fusion = bf16[6,3,128,128]{3,2,1,0:T(8,128)(2,1)S(1)} fusion(bf16[3,3,128,128]{3,2,1,0:T(8,128)(2,1)} %param.10, bf16[3,3,128,128]{3,2,1,0:T(8,128)(2,1)} %param.7), kind=kLoop, calls=%fused_computation | loop fusion | flops 294912 | bytes 1179648 | tf_op jit(solution)/shard_map/concatenate | solution.py:486
  2.4 57.0 %shard_map.109 = (bf16[32,256,128]{2,1,0:T(8,128)(2,1)S(1)}, bf16[32,256,128]{2,1,0:T(8,128)(2,1)S(1)}, f32[1152,128]{1,0:T(8,128)S(1)}, f32[1152,128]{1,0:T(8,1...) custom-call(bf16[32,256,128]{2,1,0:T(8,128)(2,1)} %bitcast.12, bf16[32,256,128]{2,1,0:T(8,128)(2,1)} %bitcast.13, ...), custom_call_target="tpu_custom_call" | custom-call | tf_op jit(solution)/shard_map/pallas_call | solution.py:479
  59.4 2.5 %shard_map.110 = (bf16[32,256,128]{2,1,0:T(8,128)(2,1)}, bf16[32,256,128]{2,1,0:T(8,128)(2,1)}, f32[9,128,128]{2,1,0:T(8,128)}, f32[9,128,128]{2,1,0:T(8,128)}, f32[1,128]{1,0:T(1,128)}, /*index=5*/f32[1,128]{1,0:T(1,128)}) custom-call(bf16[32,256,128]{2,1,0:T(8,128)(2,1)S(1)} %get-tuple-element.18.refs_0_, ...), custom_call_target="tpu_custom_call" | custom-call | tf_op jit(solution)/shard_map/pallas_call | solution.py:488

commit v8 on v7

--- a/solution.py
+++ b/solution.py
@@ -231,7 +231,7 @@
             return pltpu.make_async_remote_copy(a, b, rs.at[i, k], rr.at[i, k], device_id=dev, device_id_type=MESH)
 
         peer = (w, h ^ 1)
-        xy = [(k, (w, h ^ (2 * k))) for k in range(1, 4)]
+        xy = [(k, (w, h ^ (2 * k))) for k in (3, 2, 1)]
         zp = [(k, lax.rem(w + k, nw), lax.rem(w + nw - k, nw)) for k in range(1, nw)]
         mine = sl(core, q_me)
         pair_rs = cp(src.at[sl(1 - core, 0, half)], rd.at[i, pl.ds(0, half)], 0, peer)
@@ -399,9 +399,9 @@
                 gcat[r + 1, s, C:C2] = v
             dat[r + 2] = gcat[r + 1, :, C:C2].T
 
-    da_rows(0, 3 * th // 4)
+    da_rows(0, th // 2)
     ar_step(1, 1)
-    da_rows(3 * th // 4, th)
+    da_rows(th // 2, th)
 
     wgrad_ab(dat, ucat, dwl.at[0])
     wgrad_c(dat, ucat, dwl.at[0])

time: 62.6 us -> 62 us (level)
  no operation moved by 1% of the time
where the time goes in v8:
time: 62 us; the launch traced here: 61.6 us
  Pallas kernels  59 us (95%)
  other arithmetic  1.78 us (3%)
  between operations  0.8 us (1%)
    pallas_call x1, Pallas kernels, body(): pl.pallas_call(functools.partial(_kernel, nh, nw, th, tw), out_shape=(img...  56.4 us
    pallas_call x1, Pallas kernels, body(): pl.pallas_call(functools.partial(_flush, len(res)), out_shape=(img, img,...  2.54 us

profile of v8, /device:TPU:0, one launch (start us, length us, event | category | flops | bytes accessed | tf_op | source)
XLA Modules:
  0.0 61.6 jit_solution(5793751337510952062)
XLA Ops:
  0.6 0.7 %pad_maximum_fusion.1.gb = f32[2,128]{1,0:T(2,128)S(1)} fusion(f32[1,128]{1,0:T(1,128)} %bitcast.14, f32[1,128]{1,0:T(1,128)} %bitcast.15), kind=kLoop, calls=%fused_computation.1 | loop fusion | flops 256 | bytes 2048 | tf_op jit(solution)/shard_map/stack | solution.py:487
  1.3 1.1 %pad_maximum_fusion = bf16[6,3,128,128]{3,2,1,0:T(8,128)(2,1)S(1)} fusion(bf16[3,3,128,128]{3,2,1,0:T(8,128)(2,1)} %param.10, bf16[3,3,128,128]{3,2,1,0:T(8,128)(2,1)} %param.7), kind=kLoop, calls=%fused_computation | loop fusion | flops 294912 | bytes 1179648 | tf_op jit(solution)/shard_map/concatenate | solution.py:486
  2.4 56.4 %shard_map.109 = (bf16[32,256,128]{2,1,0:T(8,128)(2,1)S(1)}, bf16[32,256,128]{2,1,0:T(8,128)(2,1)S(1)}, f32[1152,128]{1,0:T(8,128)S(1)}, f32[1152,128]{1,0:T(8,1...) custom-call(bf16[32,256,128]{2,1,0:T(8,128)(2,1)} %bitcast.12, bf16[32,256,128]{2,1,0:T(8,128)(2,1)} %bitcast.13, ...), custom_call_target="tpu_custom_call" | custom-call | tf_op jit(solution)/shard_map/pallas_call | solution.py:479
  58.9 2.5 %shard_map.110 = (bf16[32,256,128]{2,1,0:T(8,128)(2,1)}, bf16[32,256,128]{2,1,0:T(8,128)(2,1)}, f32[9,128,128]{2,1,0:T(8,128)}, f32[9,128,128]{2,1,0:T(8,128)}, f32[1,128]{1,0:T(1,128)}, /*index=5*/f32[1,128]{1,0:T(1,128)}) custom-call(bf16[32,256,128]{2,1,0:T(8,128)(2,1)S(1)} %get-tuple-element.18.refs_0_, ...), custom_call_target="tpu_custom_call" | custom-call | tf_op jit(solution)/shard_map/pallas_call | solution.py:488
